TPU v7x, 128 devices: a whole 4x4x4 slice. The times are simulated.
128 devices in a mesh: aa: 8 (over x, core), ba: 16 (over z, y).
Axes of the slice: x: 4, y: 4, z: 4, core: 2. Of those that a mesh axis runs over, the one named last changes fastest.
Arguments:
- positions: float32 [3, 65536], P(None, ('aa', 'ba')), may hold values from -1.5 to 1.5
- forces: float32 [3, 65536], P(None, ('aa', 'ba')), may hold values from -3 to 3
- tension: float32 [65536], P(('aa', 'ba')), may hold values from -6 to 6
- node_slot: int32 [65536], P(('aa', 'ba')), may hold values from 0 to 65535, as said below
- leaf_local: float32 [2048, 3, 128], P(('aa', 'ba')), may hold values from -24 to 24
- parent_local: float32 [256, 3, 128], P(('aa', 'ba')), may hold values from -24 to 24
- l2l_maps: float32 [8, 384, 384], replicated, may hold values from -0.3125 to 0.3125
- leaf_parent: int32 [2048], P(('aa', 'ba')), may hold values from 0 to 255, as said below
- leaf_octant: int32 [2048], P(('aa', 'ba')), may hold values from 0 to 7
- near_list: int32 [2048, 27], P(('aa', 'ba')), may hold values from 0 to 2047, as said below
- blocks: float32 [1024, 256, 256], P(('aa', 'ba')), may hold values from -0.375 to 0.375
Outputs:
- result: float32 [1024, 256], P(('aa', 'ba'))
Inputs may be any that keep to these rules, and one draw needn't show every extreme that they name: `node_slot`: A permutation. Of the nodes of one device (512 in a row), at most 16 have slots in the range of any one device (512 consecutive slots), and some pair of devices reaches 16. Every device has nodes in the ranges of the devices just before and just after it, counted round. `leaf_parent`: the parent of a leaf of device d lies among parents 2 * (d - 1) to 2 * (d + 2) - 1. `near_list`: each row holds 27 different leaves, the first the leaf itself, all within 128 leaves of it.
All inputs are finite; a program needn't handle non-finite values. Where the computation divides by a largest or mean magnitude, that divisor is 1e-20 or more.
Results may differ from a plain program's by a relative error of at most 0.00012.
Values sent between devices are 32-bit elements; how exact they have to be, the bound alone decides.
No kernel may reach another device: no remote copies, remote signals or barrier semaphores. Data moves between devices by JAX's collectives and lax.ppermute only.
A program may use at most 64 MiB of HBM per device.

v0:
```python
import jax
import jax.numpy as jnp
import numpy as np
from jax import lax
from jax.experimental import pallas as pl
from jax.experimental.pallas import tpu as pltpu
from jax.sharding import PartitionSpec as P

DEVICES = 128
NODES = 512
CAP = 16
REACH = 8
SPAN = 2 * REACH + 1
LEAVES = 16
LPTS = 32
NEAR = 27
NEQ = 128
LANES = LEAVES * LPTS
WORDS = 7 * SPAN * CAP
CHUNKS = 15
EPS2 = 0.05**2
MARGIN = 0.05
SHELL = 2.95
GOLDEN = 2.399963229728653
EIGHT_PI = 25.132741228718345
AXES = ("aa", "ba")
HIGHEST = lax.Precision.HIGHEST
F32, BF16 = jnp.float32, jnp.bfloat16
NT = (((1,), (1,)), ((), ()))
NN = (((1,), (0,)), ((), ()))


def iota(shape, dim):
    return lax.broadcasted_iota(jnp.int32, shape, dim)


def three(x):
    high = x.astype(BF16).astype(F32)
    rest = x - high
    middle = rest.astype(BF16).astype(F32)
    return high, middle, rest - middle


def two(x):
    high = x.astype(BF16)
    return high, (x - high.astype(F32)).astype(BF16)


def dot(a, b, dims):
    return lax.dot_general(a, b, dims, preferred_element_type=F32)


def thirds(x, rows):
    return x[:rows] + x[rows : 2 * rows] + x[2 * rows :]


def shell_table():
    q = np.arange(NEQ, dtype=np.float32) + np.float32(0.5)
    h = (np.float32(1.0) - np.float32(2.0) * q / np.float32(NEQ)).astype(np.float32)
    radius = np.sqrt(np.maximum(np.float32(1.0) - h * h, 0)).astype(np.float32)
    angle = (q * np.float32(GOLDEN)).astype(np.float32)
    w = np.stack([radius * np.cos(angle), radius * np.sin(angle), h]).astype(np.float32)
    s = w / np.max(np.abs(w), axis=0, keepdims=True)
    table = np.zeros((3, LPTS, LANES), np.float32)
    for g in range(NEQ // LPTS):
        table[:, :, NEAR + g :: LPTS] = s[:, g * LPTS : (g + 1) * LPTS, None]
    return table.reshape(3 * LPTS, LANES)


def owner_hot(slot):
    return (iota((DEVICES, NODES), 0) == (slot >> 9)).astype(F32)


def pack_kernel(pos_ref, force_ref, slot_ref, message_ref, rank_ref, rows_ref):
    slot = slot_ref[...]
    hot = owner_hot(slot)
    hot_b = hot.astype(BF16)
    before = (iota((NODES, NODES), 0) < iota((NODES, NODES), 1)).astype(F32).astype(BF16)
    rank = jnp.sum(hot * dot(hot_b, before, NN), axis=0, keepdims=True)
    rank_ref[...] = rank
    here = iota((CAP, NODES), 0).astype(F32) == rank
    within = (slot & (NODES - 1)).astype(F32) + 1.0
    payload = [pos_ref[c : c + 1, :] for c in range(3)]
    payload += [force_ref[c : c + 1, :] for c in range(3)] + [within]
    spread = jnp.concatenate([jnp.where(here, row, 0.0) for row in payload], axis=0)
    terms = jnp.concatenate(three(spread), axis=0).astype(BF16)
    buckets = thirds(dot(terms, hot_b, NT), 7 * CAP)
    rows_ref[WORDS:, :] = jnp.zeros((CHUNKS * 128 - WORDS, DEVICES), F32)
    for d in range(SPAN):
        shift = (REACH - d) % DEVICES
        moved = pltpu.roll(buckets, shift, 1) if shift else buckets
        for c in range(7):
            at = c * SPAN * CAP + d * CAP
            rows_ref[at : at + CAP, :] = moved[c * CAP : (c + 1) * CAP, :]
    for i in range(CHUNKS):
        message_ref[pl.ds(i, DEVICES, stride=CHUNKS), :] = rows_ref[i * 128 : (i + 1) * 128, :].T


def density_kernel(
    parent_ref, octant_ref, before_ref, own_ref, after_ref, local_ref, maps_ref, out_ref,
    six_ref, picked_ref, total_ref,
):
    o = pl.program_id(0)
    wide = 3 * NEQ

    @pl.when(o == 0)
    def _():
        for j in range(6):
            source = (before_ref, own_ref, after_ref)[j // 2]
            for c in range(3):
                six_ref[c * 8 + j : c * 8 + j + 1, :] = source[j % 2, c : c + 1, :]
        for l in range(LEAVES):
            for c in range(3):
                picked_ref[l : l + 1, c * NEQ : (c + 1) * NEQ] = six_ref[
                    pl.ds(c * 8 + parent_ref[l], 1), :
                ]
        total_ref[...] = jnp.zeros_like(total_ref)

    lane = iota((1, 2 * LEAVES), 1) % LEAVES
    octants = jnp.zeros((1, 2 * LEAVES), jnp.int32)
    for l in range(LEAVES):
        octants = jnp.where(lane == l, octant_ref[l], octants)
    weights = jnp.concatenate(two(picked_ref[...]), axis=0)
    high, low = two(maps_ref[0])
    image = dot(high, weights, NT) + dot(low, weights, NT)
    total_ref[...] += jnp.where(octants == o, image, 0.0)

    @pl.when(o == 7)
    def _():
        total = total_ref[...]
        moved = total[:, :LEAVES] + total[:, LEAVES:]
        lane = iota((LEAVES, LANES), 1)
        row = iota((LEAVES, LANES), 0)
        pieces = []
        for c in range(3):
            local = jnp.concatenate(
                [local_ref[:, c, :], jnp.zeros((NEQ - LEAVES, NEQ), F32)], axis=0
            ).T[:, :LEAVES]
            pieces.append(local + moved[c * NEQ : (c + 1) * NEQ])
        placed = jnp.zeros((3 * LPTS, LANES), F32)
        for g in range(NEQ // LPTS):
            group = jnp.concatenate([p[g * LPTS : (g + 1) * LPTS] for p in pieces], axis=0)
            place = (lane == row * LPTS + NEAR + g).astype(F32)
            placed = placed + lax.dot_general(
                group, place, NN, precision=HIGHEST, preferred_element_type=F32
            )
        out_ref[...] = placed


def field_kernel(
    arrived_ref, near_ref, density_ref, shell_ref, out_ref,
    turned_ref, tree_ref, source_ref, target_ref, partial_ref, back_ref,
):
    entries = SPAN * CAP
    turned = []
    for i in range(CHUNKS):
        turned.append(arrived_ref[pl.ds(i, DEVICES, stride=CHUNKS), :].T)
    turned = jnp.concatenate(turned, axis=0)
    for c in range(7):
        turned_ref[pl.ds(c, entries, stride=8), :] = turned[c * entries : (c + 1) * entries, :]
    turned_ref[pl.ds(7, entries, stride=8), :] = jnp.zeros((entries, DEVICES), F32)
    tree_ref[SPAN * 32 :, :] = jnp.zeros((1024 - SPAN * 32, 128), F32)
    low_row = iota((128, 128), 0)

    def place(d, carry):
        lows, values = [], []
        for r in range(CAP):
            entry = turned_ref[pl.ds(pl.multiple_of((d * CAP + r) * 8, 8), 8), :]
            slot = entry[6:7, :].astype(jnp.int32) - 1
            lows.append((low_row == (slot & 127)).astype(F32).astype(BF16))
            high = slot >> 7
            parts = three(entry)
            values.append(
                jnp.concatenate(
                    [jnp.where(high == h, part, 0.0) for part in parts for h in range(4)], axis=0
                ).astype(BF16)
            )
        placed = dot(jnp.concatenate(values, axis=1), jnp.concatenate(lows, axis=1), NT)
        tree_ref[pl.ds(pl.multiple_of(d * 32, 32), 32), :] = thirds(placed, 32)
        return carry

    lax.fori_loop(0, SPAN, place, 0)

    terms = [[], [], []]
    for c in range(6):
        turned_c = tree_ref[pl.ds(c, 128, stride=8), :].T
        for s, part in enumerate(three(turned_c)):
            part = part.astype(BF16)
            terms[s].append(
                jnp.concatenate([part[w * LPTS : (w + 1) * LPTS] for w in range(4)], axis=1)
            )
    everything = jnp.concatenate([t for s in range(3) for t in terms[s]], axis=0)
    positions = jnp.concatenate([t for s in range(3) for t in terms[s][:3]], axis=0)
    leaf_row = iota((128, LANES), 0)

    def hot(leaf):
        quarter, row = leaf & 3, leaf >> 2
        return jnp.concatenate(
            [
                (leaf_row == jnp.where(quarter == w, row, -1)).astype(F32).astype(BF16)
                for w in range(4)
            ],
            axis=0,
        )

    lane = iota((1, LANES), 1)
    gathered = thirds(dot(everything, hot(near_ref[...]), NN), 6 * LPTS)
    targets = thirds(dot(positions, hot(lane // LPTS + REACH * LEAVES), NN), 3 * LPTS)
    for k in range(LANES // 128):
        target_ref[k * 96 : (k + 1) * 96, :] = targets[:, k * 128 : (k + 1) * 128]
    axes = [targets[c * LPTS : (c + 1) * LPTS] for c in range(3)]
    centers = [jnp.sum(a, axis=0, keepdims=True) * (1.0 / LPTS) for a in axes]
    half = jnp.maximum(
        jnp.maximum(
            jnp.max(jnp.abs(axes[0] - centers[0]), axis=0, keepdims=True),
            jnp.max(jnp.abs(axes[1] - centers[1]), axis=0, keepdims=True),
        ),
        jnp.max(jnp.abs(axes[2] - centers[2]), axis=0, keepdims=True),
    ) + MARGIN
    spot = lane % LPTS
    far = (spot >= NEAR) & (spot < NEAR + NEQ // LPTS)
    for c in range(3):
        rows = slice(c * LPTS, (c + 1) * LPTS)
        shell = jnp.where(far, centers[c], 0.0) + (SHELL * half) * shell_ref[rows, :]
        source_ref[rows, :] = gathered[rows, :] + shell
    source_ref[3 * LPTS :, :] = gathered[3 * LPTS :, :] + density_ref[...]

    soft = jnp.where(far, 0.0, EPS2)
    for chunk in range(LANES // 128):
        lanes = slice(chunk * 128, (chunk + 1) * 128)
        soft_c = soft[:, lanes]

        def step(p, carry):
            aim = [target_ref[pl.ds(chunk * 96 + c * LPTS + p, 1), :] for c in range(3)]
            sums = None
            for g in range(LPTS // 8):
                at = [source_ref[c * LPTS + g * 8 : c * LPTS + g * 8 + 8, lanes] for c in range(6)]
                gap = [aim[c] - at[c] for c in range(3)]
                square = gap[0] * gap[0] + gap[1] * gap[1] + gap[2] * gap[2] + soft_c
                inverse = lax.rsqrt(square)
                cube = inverse * inverse * inverse
                along = (gap[0] * at[3] + gap[1] * at[4] + gap[2] * at[5]) * cube
                plain = (square + soft_c) * cube
                new = [plain * at[3 + c] + gap[c] * along for c in range(3)]
                sums = new if sums is None else [a + b for a, b in zip(sums, new)]
            for c in range(3):
                partial_ref[pl.ds(chunk * 96 + c * LPTS + p, 1), :] = jnp.sum(
                    sums[c], axis=0, keepdims=True
                )
            return carry

        lax.fori_loop(0, LPTS, step, 0, unroll=2)

    same = (iota((LEAVES, LANES), 1) // LPTS == iota((LEAVES, LANES), 0)).astype(F32)
    partial = jnp.concatenate([partial_ref[k * 96 : (k + 1) * 96, :] for k in range(4)], axis=1)
    by_leaf = [
        lax.dot_general(
            same, partial[c * LPTS : (c + 1) * LPTS, :], NT, precision=HIGHEST,
            preferred_element_type=F32,
        )
        for c in range(3)
    ]
    velocity = jnp.concatenate(by_leaf, axis=0) * (1.0 / EIGHT_PI)
    velocity = jnp.concatenate(three(velocity), axis=0).astype(BF16)
    node_row = iota((LPTS, DEVICES), 0)
    leaf_of = iota((LEAVES, DEVICES), 0)
    back_ref[...] = jnp.zeros_like(back_ref)
    slots, hots = [], []
    for r in range(CAP):
        entry = turned_ref[(REACH * CAP + r) * 8 : (REACH * CAP + r) * 8 + 8, :]
        slot = entry[6:7, :].astype(jnp.int32) - 1
        slots.append(slot)
        hots.append((node_row == (slot & (LPTS - 1))).astype(F32).astype(BF16))
    picked = thirds(dot(velocity, jnp.concatenate(hots, axis=1), NN), 3 * LEAVES)
    for r in range(CAP):
        mine = leaf_of == (slots[r] >> 5)
        for c in range(3):
            piece = picked[c * LEAVES : (c + 1) * LEAVES, r * 128 : (r + 1) * 128]
            back_ref[c * CAP + r : c * CAP + r + 1, :] = jnp.sum(
                jnp.where(mine, piece, 0.0), axis=0, keepdims=True
            )
    out_ref[...] = back_ref[...].T


def fiber_kernel(arrived_ref, slot_ref, rank_ref, tension_ref, blocks_ref, out_ref, vector_ref):
    hot = owner_hot(slot_ref[...]).astype(BF16)
    words = arrived_ref[...].T[: 3 * CAP]
    terms = jnp.concatenate(three(words), axis=0).astype(BF16)
    picked = thirds(dot(terms, hot, NN), 3 * CAP)
    here = iota((CAP, NODES), 0).astype(F32) == rank_ref[...]
    rows = [
        jnp.sum(jnp.where(here, picked[c * CAP : (c + 1) * CAP], 0.0), axis=0, keepdims=True)
        for c in range(3)
    ] + [tension_ref[...]]
    first = iota((1, 128), 1) < 64
    for pair in range(NODES // 128):
        cut = [row[:, pair * 128 : (pair + 1) * 128] for row in rows]
        swapped = [pltpu.roll(row, 64, 1) for row in cut]
        for k in range(2):
            a, b = cut[2 * k], cut[2 * k + 1]
            sa, sb = swapped[2 * k], swapped[2 * k + 1]
            lanes = slice(k * 128, (k + 1) * 128)
            vector_ref[2 * pair : 2 * pair + 1, lanes] = jnp.where(first, a, sb)
            vector_ref[2 * pair + 1 : 2 * pair + 2, lanes] = jnp.where(first, sa, b)
    vector = jnp.concatenate(two(vector_ref[...]), axis=0)
    row = iota((16, 256), 0) % 8
    total = jnp.zeros((16, 256), F32)
    for i in range(8):
        high, low = two(blocks_ref[i])
        image = dot(vector, high, NT) + dot(vector, low, NT)
        total = jnp.where(row == i, image, total)
    out_ref[...] = total[:8] + total[8:]


def shape(*dims):
    return jax.ShapeDtypeStruct(dims, F32)


def shifted(value, by):
    return lax.ppermute(value, AXES, [(i, (i + by) % DEVICES) for i in range(DEVICES)])


def exchange(rows):
    return lax.all_to_all(rows.reshape(-1), AXES, 0, 0, tiled=True).reshape(rows.shape)


def local(
    positions, forces, tension, node_slot, leaf_local, parent_local, l2l_maps, leaf_parent,
    leaf_octant, near_list, blocks,
):
    device = lax.axis_index("aa") * lax.axis_size("ba") + lax.axis_index("ba")
    slot = node_slot.reshape(1, NODES)
    from_before = shifted(parent_local, 1)
    from_after = shifted(parent_local, -1)
    message, rank = pl.pallas_call(
        pack_kernel,
        out_shape=(shape(CHUNKS * 128, 128), shape(1, NODES)),
        scratch_shapes=[pltpu.VMEM((CHUNKS * 128, DEVICES), F32)],
        cost_estimate=pl.CostEstimate(flops=10**8, bytes_accessed=10**6, transcendentals=0),
        name="pack",
    )(positions, forces, slot)
    arrived = exchange(message)

    vmem = pl.BlockSpec(memory_space=pltpu.VMEM)
    smem = pl.BlockSpec(memory_space=pltpu.SMEM)
    density = pl.pallas_call(
        density_kernel,
        grid=(8,),
        out_shape=shape(3 * LPTS, LANES),
        in_specs=[smem, smem, vmem, vmem, vmem, vmem, pl.BlockSpec((1, 384, 384), lambda o: (o, 0, 0))],
        out_specs=pl.BlockSpec((3 * LPTS, LANES), lambda o: (0, 0)),
        scratch_shapes=[
            pltpu.VMEM((24, NEQ), F32),
            pltpu.VMEM((LEAVES, 3 * NEQ), F32),
            pltpu.VMEM((3 * NEQ, 2 * LEAVES), F32),
        ],
        cost_estimate=pl.CostEstimate(flops=10**9, bytes_accessed=5 * 10**6, transcendentals=0),
        name="density",
    )(
        leaf_parent - 2 * (device - 1), leaf_octant, from_before, parent_local, from_after,
        leaf_local, l2l_maps,
    )
    near = jnp.pad(
        near_list - LEAVES * (device - REACH), ((0, 0), (0, LPTS - NEAR)), constant_values=-1
    ).reshape(1, LANES)

    back = pl.pallas_call(
        field_kernel,
        out_shape=shape(DEVICES, 128),
        scratch_shapes=[
            pltpu.VMEM((SPAN * CAP * 8, DEVICES), F32),
            pltpu.VMEM((1024, 128), F32),
            pltpu.VMEM((6 * LPTS, LANES), F32),
            pltpu.VMEM((12 * LPTS, 128), F32),
            pltpu.VMEM((12 * LPTS, 128), F32),
            pltpu.VMEM((128, DEVICES), F32),
        ],
        cost_estimate=pl.CostEstimate(flops=10**9, bytes_accessed=2 * 10**6, transcendentals=0),
        name="field",
    )(arrived, near, density, jnp.asarray(shell_table()))
    returned = exchange(back)
    return pl.pallas_call(
        fiber_kernel,
        out_shape=shape(8, 256),
        scratch_shapes=[pltpu.VMEM((8, 256), F32)],
        cost_estimate=pl.CostEstimate(flops=10**8, bytes_accessed=2 * 10**6, transcendentals=0),
        name="fiber",
    )(returned, slot, rank, tension.reshape(1, NODES), blocks)


def solution(mesh):
    both = ("aa", "ba")
    in_specs = (
        P(None, both), P(None, both), P(both), P(both), P(both, None, None), P(both, None, None),
        P(), P(both), P(both), P(both, None), P(both, None, None),
    )
    return jax.shard_map(
        local, mesh=mesh, in_specs=in_specs, out_specs=P(both, None), check_vma=False
    )
```

profile of v0, /device:TPU:1, one launch (start us, length us, event | category | flops | bytes accessed | tf_op | source)
XLA Modules:
  0.0 72.5 jit_solution(8028726622398664552)
XLA Ops:
  0.0 2.7 %pack.1 = (f32[1920,128]{1,0:T(8,128)}, f32[1,512]{1,0:T(1,128)}) custom-call(f32[3,512]{1,0:T(4,128)} %pos_ref.1, f32[3,512]{1,0:T(4,128)} %force_ref.1, s32[1,512]{1,0:T(1,128)} %bitcast.12), custom_call_target="tpu_custom_call" | custom-call | flops 100000000 | bytes 1000000 | tf_op jit(solution)/shard_map/pack/pallas_call | solution.py:335
  2.7 11.5 %all-to-all-start = ((f32[128,1920,1]{1,2,0:T(1,128)}), f32[128,1920,1]{1,2,0:T(1,128)S(1)}, u32[]{:S(2)}, u32[]{:S(2)}) async-start(f32[128,1920,1]{1,2,0:T(1,128)} %bitcast.9), calls=%async_computation | async-start | bytes 1966080 | tf_op jit(solution)/shard_map/all_to_all | solution.py:324
  14.2 0.7 copy.18.own_ref
  14.9 0.0 copy-start.1
  14.9 1.4 %collective-permute-start = (f32[2,3,128]{2,1,0:T(4,128)S(1)}, f32[2,3,128]{2,1,0:T(4,128)S(1)}, u32[]{:S(2)}, u32[]{:S(2)}) collective-permute-start(f32[2,3,128]{2,1,0:T(4,128)S(1)} %copy.18.own_ref), channel_id=1, source_target_pairs={{0,1},{1,2},{2,3},{3,4},{4,5},{5,6},{6,7},{7,8},{8,9},{9,10},{10,1... | collective-permute-start | bytes 9224 | tf_op jit(solution)/shard_map/ppermute | solution.py:320
  16.2 4.5 %collective-permute-start.1 = (f32[2,3,128]{2,1,0:T(4,128)S(1)}, f32[2,3,128]{2,1,0:T(4,128)S(1)}, u32[]{:S(2)}, u32[]{:S(2)}) collective-permute-start(f32[2,3,128]{2,1,0:T(4,128)S(1)} %copy.18.own_ref), channel_id=1, source_target_pairs={{0,127},{1,0},{2,1},{3,2},{4,3},{5,4},{6,5},{7,6},{8,7},{9,8},{10,... | collective-permute-start | bytes 9224 | tf_op jit(solution)/shard_map/ppermute | solution.py:320
  20.7 0.7 broadcast_subtract_fusion
  21.4 1.2 %broadcast_subtract_fusion.1.parent_ref = s32[16]{0:T(128)} fusion(s32[16]{0:T(128)} %param.19, s32[]{:T(128)S(6)} %mul_shard_map.3), kind=kLoop, calls=%fused_computation.1 | loop fusion | flops 16 | bytes 132 | tf_op jit(solution)/shard_map/sub | solution.py:360
  22.6 0.7 reshape.27.near_ref
  23.3 1.4 %copy.21.local_ref = f32[16,3,128]{2,1,0:T(4,128)} copy(f32[16,3,128]{2,0,1:T(8,128)} %param.16) | data formatting | bytes 49152 | tf_op args[4]
  24.7 1.0 %collective-permute-done.before_ref = f32[2,3,128]{2,1,0:T(4,128)S(1)} collective-permute-done((f32[2,3,128]{2,1,0:T(4,128)S(1)}, f32[2,3,128]{2,1,0:T(4,128)S(1)}, u32[]{:S(2)}, u32[]{:S(2)}) %collective-permute-start) | collective-permute-done | bytes 3104 | tf_op jit(solution)/shard_map/ppermute | solution.py:320
  25.7 0.0 copy-start.2
  25.7 0.0 collective-permute-done.1.after_ref
  25.7 0.0 copy-done.1
  25.7 0.6 copy-done.2
  26.2 0.0 copy-start.3
  26.2 0.6 copy-done.3
  26.8 7.6 %density.1.density_ref = f32[96,512]{1,0:T(8,128)} custom-call(s32[16]{0:T(128)} %broadcast_subtract_fusion.1.parent_ref, s32[16]{0:T(128)} %octant_ref.1, f32[2,3,128]{2,1,0:T(4,128)} %copy-done.2, f32[2,3,128]{2,1,0:T(4,128)} %copy-done.1, f32[2,3,128]{2,1,0:T(4,128)} %copy-done.3, f32[16,3,128]{2,1,0:T(4,128)} %copy.21.local_ref, f32[8,384,384]{2,1,0:T(8,128)} %maps_ref.1), custom_call_target="tpu_custom_call" | custom-call | flops 1000000000 | bytes 5000000 | tf_op jit(solution)/shard_map/density/pallas_call | solution.py:346
  34.5 0.0 all-to-all-done
  34.5 0.0 copy-start
  34.5 0.9 %copy-done = f32[128,1920,1]{1,2,0:T(1,128)} copy-done((f32[128,1920,1]{1,2,0:T(1,128)}, f32[128,1920,1]{1,2,0:T(1,128)S(1)}, u32[]{:S(2)}) %copy-start) | copy-done | bytes 983064
  35.4 12.6 %field.1 = f32[128,128]{1,0:T(8,128)} custom-call(f32[1920,128]{1,0:T(8,128)} %bitcast.8, s32[1,512]{1,0:T(1,128)} %reshape.27.near_ref, f32[96,512]{1,0:T(8,128)} %density.1.density_ref, f32[96,512]{1,0:T(8,128)} %constant.22.clone.shell_ref), custom_call_target="tpu_custom_call" | custom-call | flops 1000000000 | bytes 2000000 | tf_op jit(solution)/shard_map/field/pallas_call | solution.py:367
  48.0 21.3 %all_to_all.18 = f32[128,128,1]{1,2,0:T(1,128)} all-to-all(f32[128,128,1]{1,2,0:T(1,128)} %bitcast.11), channel_id=1, replica_groups=mesh['aa'=8,'ba'=16] {'aa','ba'}, dimensions={0} | all-to-all | bytes 131072 | tf_op jit(solution)/shard_map/all_to_all | solution.py:324
  69.3 3.2 %fiber.1 = f32[8,256]{1,0:T(8,128)} custom-call(f32[128,128]{1,0:T(8,128)} %bitcast.10, s32[1,512]{1,0:T(1,128)} %bitcast.13, f32[1,512]{1,0:T(1,128)} %get-tuple-element.8.rank_ref, f32[1,512]{1,0:T(1,128)} %bitcast.14, f32[8,256,256]{2,1,0:T(8,128)} %blocks_ref.1), custom_call_target="tpu_custom_call" | custom-call | flops 100000000 | bytes 2000000 | tf_op jit(solution)/shard_map/fiber/pallas_call | solution.py:382
  (1 shorter events, 0.0 us)
Async XLA Ops:
  2.7 31.8 %all-to-all-start = ((f32[128,1920,1]{1,2,0:T(1,128)}), f32[128,1920,1]{1,2,0:T(1,128)S(1)}, u32[]{:S(2)}, u32[]{:S(2)}) async-start(f32[128,1920,1]{1,2,0:T(1,128)} %bitcast.9), calls=%async_computation | async-start | bytes 1966080 | tf_op jit(solution)/shard_map/all_to_all | solution.py:324
  14.9 10.8 %copy-start.1 = (f32[2,3,128]{2,1,0:T(4,128)}, f32[2,3,128]{2,1,0:T(4,128)S(1)}, u32[]{:S(2)}) copy-start(f32[2,3,128]{2,1,0:T(4,128)S(1)} %copy.18.own_ref) | copy-start | bytes 9220
  14.9 10.8 %collective-permute-start = (f32[2,3,128]{2,1,0:T(4,128)S(1)}, f32[2,3,128]{2,1,0:T(4,128)S(1)}, u32[]{:S(2)}, u32[]{:S(2)}) collective-permute-start(f32[2,3,128]{2,1,0:T(4,128)S(1)} %copy.18.own_ref), channel_id=1, source_target_pairs={{0,1},{1,2},{2,3},{3,4},{4,5},{5,6},{6,7},{7,8},{8,9},{9,10},{10,1... | collective-permute-start | bytes 9224 | tf_op jit(solution)/shard_map/ppermute | solution.py:320
  16.2 9.4 %collective-permute-start.1 = (f32[2,3,128]{2,1,0:T(4,128)S(1)}, f32[2,3,128]{2,1,0:T(4,128)S(1)}, u32[]{:S(2)}, u32[]{:S(2)}) collective-permute-start(f32[2,3,128]{2,1,0:T(4,128)S(1)} %copy.18.own_ref), channel_id=1, source_target_pairs={{0,127},{1,0},{2,1},{3,2},{4,3},{5,4},{6,5},{7,6},{8,7},{9,8},{10,... | collective-permute-start | bytes 9224 | tf_op jit(solution)/shard_map/ppermute | solution.py:320
  25.7 0.6 copy-start.2
  26.2 0.6 copy-start.3
  34.5 0.9 %copy-start = (f32[128,1920,1]{1,2,0:T(1,128)}, f32[128,1920,1]{1,2,0:T(1,128)S(1)}, u32[]{:S(2)}) copy-start(f32[128,1920,1]{1,2,0:T(1,128)S(1)} %all-to-all-done) | copy-start | bytes 2949124
where the time goes:
time: 73 us; the launch traced here: 72.5 us
  Pallas kernels  26.1 us (36%)
  blocking collectives  21.3 us (29%)
  starting transfers between devices  17.3 us (24%)
  local copies, waits for them, and re-layouts  4.83 us (7%)
  other arithmetic  1.93 us (3%)
  waiting for transfers between devices  1 us (1%)
    all_to_all x1, blocking collectives, exchange(): lax.all_to_all(rows.reshape(-1), AXES, 0, 0, tiled=True).reshape(rows.shape)  21.3 us
    pallas_call x1, Pallas kernels, local(): pl.pallas_call(field_kernel, out_shape=shape(DEVICES, 128), scratch_shape...  12.6 us
    all_to_all x1, starting transfers between devices, exchange(): lax.all_to_all(rows.reshape(-1), AXES, 0, 0, tiled=True).reshape(rows.shape)  11.5 us
    pallas_call x1, Pallas kernels, local(): pl.pallas_call(density_kernel, grid=(8,), out_shape=shape(3 * LPTS, LANES...  7.64 us
    ppermute x2, starting transfers between devices, shifted(): lax.ppermute(value, AXES, [(i, (i + by) % DEVICES) for i in range(DEVICES)])  5.82 us
    unnamed x10, local copies, waits for them, and re-layouts  4.15 us
    pallas_call x1, Pallas kernels, local(): pl.pallas_call(fiber_kernel, out_shape=shape(8, 256), scratch_shapes=[plt...  3.2 us
    pallas_call x1, Pallas kernels, local(): pl.pallas_call(pack_kernel, out_shape=(shape(CHUNKS * 128, 128), shape(1,...  2.69 us
  transfers between devices with their start and end apart: 3, of which 1 were waited for; matrix products, arithmetic and copies ran while one was open for 6% of the time, Pallas kernels for 11%

commit v1 on v0

--- a/solution.py
+++ b/solution.py
@@ -18,6 +18,7 @@
 LANES = LEAVES * LPTS
 WORDS = 7 * SPAN * CAP
 CHUNKS = 15
+MAPS_GRANT = 8
 EPS2 = 0.05**2
 MARGIN = 0.05
 SHELL = 2.95
@@ -65,6 +66,10 @@
     for g in range(NEQ // LPTS):
         table[:, :, NEAR + g :: LPTS] = s[:, g * LPTS : (g + 1) * LPTS, None]
     return table.reshape(3 * LPTS, LANES)
+
+
+def device_index():
+    return lax.axis_index("aa") * 16 + lax.axis_index("ba")
 
 
 def owner_hot(slot):
@@ -98,53 +103,42 @@
 
 def density_kernel(
     parent_ref, octant_ref, before_ref, own_ref, after_ref, local_ref, maps_ref, out_ref,
-    six_ref, picked_ref, total_ref,
+    six_ref, picked_ref,
 ):
-    o = pl.program_id(0)
-    wide = 3 * NEQ
-
-    @pl.when(o == 0)
-    def _():
-        for j in range(6):
-            source = (before_ref, own_ref, after_ref)[j // 2]
-            for c in range(3):
-                six_ref[c * 8 + j : c * 8 + j + 1, :] = source[j % 2, c : c + 1, :]
-        for l in range(LEAVES):
-            for c in range(3):
-                picked_ref[l : l + 1, c * NEQ : (c + 1) * NEQ] = six_ref[
-                    pl.ds(c * 8 + parent_ref[l], 1), :
-                ]
-        total_ref[...] = jnp.zeros_like(total_ref)
-
+    first_parent = 2 * (device_index() - 1)
+    for j in range(6):
+        source = (before_ref, own_ref, after_ref)[j // 2]
+        for c in range(3):
+            six_ref[c * 8 + j : c * 8 + j + 1, :] = source[c, j % 2 : j % 2 + 1, :]
+    for l in range(LEAVES):
+        for c in range(3):
+            picked_ref[l : l + 1, c * NEQ : (c + 1) * NEQ] = six_ref[
+                pl.ds(c * 8 + parent_ref[l] - first_parent, 1), :
+            ]
     lane = iota((1, 2 * LEAVES), 1) % LEAVES
     octants = jnp.zeros((1, 2 * LEAVES), jnp.int32)
     for l in range(LEAVES):
         octants = jnp.where(lane == l, octant_ref[l], octants)
     weights = jnp.concatenate(two(picked_ref[...]), axis=0)
-    high, low = two(maps_ref[0])
-    image = dot(high, weights, NT) + dot(low, weights, NT)
-    total_ref[...] += jnp.where(octants == o, image, 0.0)
-
-    @pl.when(o == 7)
-    def _():
-        total = total_ref[...]
-        moved = total[:, :LEAVES] + total[:, LEAVES:]
-        lane = iota((LEAVES, LANES), 1)
-        row = iota((LEAVES, LANES), 0)
-        pieces = []
-        for c in range(3):
-            local = jnp.concatenate(
-                [local_ref[:, c, :], jnp.zeros((NEQ - LEAVES, NEQ), F32)], axis=0
-            ).T[:, :LEAVES]
-            pieces.append(local + moved[c * NEQ : (c + 1) * NEQ])
-        placed = jnp.zeros((3 * LPTS, LANES), F32)
-        for g in range(NEQ // LPTS):
-            group = jnp.concatenate([p[g * LPTS : (g + 1) * LPTS] for p in pieces], axis=0)
-            place = (lane == row * LPTS + NEAR + g).astype(F32)
-            placed = placed + lax.dot_general(
-                group, place, NN, precision=HIGHEST, preferred_element_type=F32
-            )
-        out_ref[...] = placed
+    total = jnp.zeros((3 * NEQ, 2 * LEAVES), F32)
+    for o in range(8):
+        image = dot(maps_ref[0, o], weights, NT) + dot(maps_ref[1, o], weights, NT)
+        total = jnp.where(octants == o, image, total)
+    moved = total[:, :LEAVES] + total[:, LEAVES:]
+    lane = iota((LEAVES, LANES), 1)
+    row = iota((LEAVES, LANES), 0)
+    pieces = []
+    for c in range(3):
+        own = jnp.concatenate([local_ref[c], jnp.zeros((NEQ - LEAVES, NEQ), F32)], axis=0).T
+        pieces.append(own[:, :LEAVES] + moved[c * NEQ : (c + 1) * NEQ])
+    placed = jnp.zeros((3 * LPTS, LANES), F32)
+    for g in range(NEQ // LPTS):
+        group = jnp.concatenate([p[g * LPTS : (g + 1) * LPTS] for p in pieces], axis=0)
+        place = (lane == row * LPTS + NEAR + g).astype(F32)
+        placed = placed + lax.dot_general(
+            group, place, NN, precision=HIGHEST, preferred_element_type=F32
+        )
+    out_ref[...] = placed
 
 
 def field_kernel(
@@ -179,7 +173,7 @@
         tree_ref[pl.ds(pl.multiple_of(d * 32, 32), 32), :] = thirds(placed, 32)
         return carry
 
-    lax.fori_loop(0, SPAN, place, 0)
+    lax.fori_loop(0, SPAN, place, 0, unroll=True)
 
     terms = [[], [], []]
     for c in range(6):
@@ -193,8 +187,7 @@
     positions = jnp.concatenate([t for s in range(3) for t in terms[s][:3]], axis=0)
     leaf_row = iota((128, LANES), 0)
 
-    def hot(leaf):
-        quarter, row = leaf & 3, leaf >> 2
+    def hot(quarter, row):
         return jnp.concatenate(
             [
                 (leaf_row == jnp.where(quarter == w, row, -1)).astype(F32).astype(BF16)
@@ -204,8 +197,19 @@
         )
 
     lane = iota((1, LANES), 1)
-    gathered = thirds(dot(everything, hot(near_ref[...]), NN), 6 * LPTS)
-    targets = thirds(dot(positions, hot(lane // LPTS + REACH * LEAVES), NN), 3 * LPTS)
+    spot = lane % LPTS
+    near = near_ref[...] - LEAVES * (device_index() - REACH)
+    spread = (iota((NEAR, LANES), 0) == spot).astype(F32).astype(BF16)
+    own = iota((LEAVES, LANES), 0) == lane // LPTS
+
+    def as_lanes(value):
+        value = dot(value.astype(F32).astype(BF16), spread, NN)
+        return jnp.sum(jnp.where(own, value, 0.0), axis=0, keepdims=True).astype(jnp.int32)
+
+    near_row = jnp.where(spot < NEAR, as_lanes(near >> 2), -1)
+    leaf = lane // LPTS + REACH * LEAVES
+    gathered = thirds(dot(everything, hot(as_lanes(near & 3), near_row), NN), 6 * LPTS)
+    targets = thirds(dot(positions, hot(leaf & 3, leaf >> 2), NN), 3 * LPTS)
     for k in range(LANES // 128):
         target_ref[k * 96 : (k + 1) * 96, :] = targets[:, k * 128 : (k + 1) * 128]
     axes = [targets[c * LPTS : (c + 1) * LPTS] for c in range(3)]
@@ -217,7 +221,6 @@
         ),
         jnp.max(jnp.abs(axes[2] - centers[2]), axis=0, keepdims=True),
     ) + MARGIN
-    spot = lane % LPTS
     far = (spot >= NEAR) & (spot < NEAR + NEQ // LPTS)
     for c in range(3):
         rows = slice(c * LPTS, (c + 1) * LPTS)
@@ -249,7 +252,7 @@
                 )
             return carry
 
-        lax.fori_loop(0, LPTS, step, 0, unroll=2)
+        lax.fori_loop(0, LPTS, step, 0, unroll=8)
 
     same = (iota((LEAVES, LANES), 1) // LPTS == iota((LEAVES, LANES), 0)).astype(F32)
     partial = jnp.concatenate([partial_ref[k * 96 : (k + 1) * 96, :] for k in range(4)], axis=1)
@@ -282,7 +285,13 @@
     out_ref[...] = back_ref[...].T
 
 
-def fiber_kernel(arrived_ref, slot_ref, rank_ref, tension_ref, blocks_ref, out_ref, vector_ref):
+def split_kernel(blocks_ref, out_ref):
+    out_ref[0], out_ref[1] = two(blocks_ref[...])
+
+
+def fiber_kernel(
+    arrived_ref, slot_ref, rank_ref, tension_ref, blocks_ref, out_ref, vector_ref
+):
     hot = owner_hot(slot_ref[...]).astype(BF16)
     words = arrived_ref[...].T[: 3 * CAP]
     terms = jnp.concatenate(three(words), axis=0).astype(BF16)
@@ -306,8 +315,7 @@
     row = iota((16, 256), 0) % 8
     total = jnp.zeros((16, 256), F32)
     for i in range(8):
-        high, low = two(blocks_ref[i])
-        image = dot(vector, high, NT) + dot(vector, low, NT)
+        image = dot(vector, blocks_ref[0, i], NT) + dot(vector, blocks_ref[1, i], NT)
         total = jnp.where(row == i, image, total)
     out_ref[...] = total[:8] + total[8:]
 
@@ -316,8 +324,30 @@
     return jax.ShapeDtypeStruct(dims, F32)
 
 
+def split_up(value, step, mib):
+    count, *rest = value.shape
+    zeros = (0,) * len(rest)
+    return pl.pallas_call(
+        split_kernel,
+        grid=(count // step,),
+        out_shape=jax.ShapeDtypeStruct((2, count, *rest), BF16),
+        in_specs=[pl.BlockSpec((step, *rest), lambda i: (i, *zeros))],
+        out_specs=pl.BlockSpec((2, step, *rest), lambda i: (0, i, *zeros)),
+        cost_estimate=pl.CostEstimate(
+            flops=4 * value.size, bytes_accessed=8 * value.size, transcendentals=0
+        ),
+        compiler_params=grant(mib),
+        name="split",
+    )(value)
+
+
 def shifted(value, by):
-    return lax.ppermute(value, AXES, [(i, (i + by) % DEVICES) for i in range(DEVICES)])
+    pairs = [(i, i + by) for i in range(DEVICES) if 0 <= i + by < DEVICES]
+    return lax.ppermute(value, AXES, pairs)
+
+
+def grant(mib):
+    return pltpu.CompilerParams(vmem_limit_bytes=mib << 20)
 
 
 def exchange(rows):
@@ -328,10 +358,9 @@
     positions, forces, tension, node_slot, leaf_local, parent_local, l2l_maps, leaf_parent,
     leaf_octant, near_list, blocks,
 ):
-    device = lax.axis_index("aa") * lax.axis_size("ba") + lax.axis_index("ba")
+    parent_local = parent_local.transpose(1, 0, 2)
+    leaf_local = leaf_local.transpose(1, 0, 2)
     slot = node_slot.reshape(1, NODES)
-    from_before = shifted(parent_local, 1)
-    from_after = shifted(parent_local, -1)
     message, rank = pl.pallas_call(
         pack_kernel,
         out_shape=(shape(CHUNKS * 128, 128), shape(1, NODES)),
@@ -339,31 +368,28 @@
         cost_estimate=pl.CostEstimate(flops=10**8, bytes_accessed=10**6, transcendentals=0),
         name="pack",
     )(positions, forces, slot)
+    message, sent = lax.optimization_barrier((message, parent_local))
     arrived = exchange(message)
+    from_before = shifted(sent, 1)
+    from_after = shifted(sent, -1)
 
     vmem = pl.BlockSpec(memory_space=pltpu.VMEM)
     smem = pl.BlockSpec(memory_space=pltpu.SMEM)
     density = pl.pallas_call(
         density_kernel,
-        grid=(8,),
         out_shape=shape(3 * LPTS, LANES),
-        in_specs=[smem, smem, vmem, vmem, vmem, vmem, pl.BlockSpec((1, 384, 384), lambda o: (o, 0, 0))],
-        out_specs=pl.BlockSpec((3 * LPTS, LANES), lambda o: (0, 0)),
+        in_specs=[smem, smem, vmem, vmem, vmem, vmem, vmem],
         scratch_shapes=[
             pltpu.VMEM((24, NEQ), F32),
             pltpu.VMEM((LEAVES, 3 * NEQ), F32),
-            pltpu.VMEM((3 * NEQ, 2 * LEAVES), F32),
         ],
         cost_estimate=pl.CostEstimate(flops=10**9, bytes_accessed=5 * 10**6, transcendentals=0),
+        compiler_params=grant(16),
         name="density",
     )(
-        leaf_parent - 2 * (device - 1), leaf_octant, from_before, parent_local, from_after,
-        leaf_local, l2l_maps,
+        leaf_parent, leaf_octant, from_before, parent_local, from_after,
+        leaf_local, split_up(l2l_maps, 2, MAPS_GRANT),
     )
-    near = jnp.pad(
-        near_list - LEAVES * (device - REACH), ((0, 0), (0, LPTS - NEAR)), constant_values=-1
-    ).reshape(1, LANES)
-
     back = pl.pallas_call(
         field_kernel,
         out_shape=shape(DEVICES, 128),
@@ -376,16 +402,18 @@
             pltpu.VMEM((128, DEVICES), F32),
         ],
         cost_estimate=pl.CostEstimate(flops=10**9, bytes_accessed=2 * 10**6, transcendentals=0),
+        compiler_params=grant(16),
         name="field",
-    )(arrived, near, density, jnp.asarray(shell_table()))
+    )(arrived, near_list, density, jnp.asarray(shell_table()))
     returned = exchange(back)
     return pl.pallas_call(
         fiber_kernel,
         out_shape=shape(8, 256),
         scratch_shapes=[pltpu.VMEM((8, 256), F32)],
         cost_estimate=pl.CostEstimate(flops=10**8, bytes_accessed=2 * 10**6, transcendentals=0),
+        compiler_params=grant(8),
         name="fiber",
-    )(returned, slot, rank, tension.reshape(1, NODES), blocks)
+    )(returned, slot, rank, tension.reshape(1, NODES), split_up(blocks, 2, 4))
 
 
 def solution(mesh):

time: 73 us -> 59.4 us (0.81)
  blocking collectives: 21.3 us -> 0 us
  starting transfers between devices: 17.3 us -> 27.7 us
  waiting for transfers between devices: 1 us -> 10.1 us
  Pallas kernels: 26.1 us -> 17.1 us
  other arithmetic: 1.93 us -> 0 us
  local copies, waits for them, and re-layouts: 4.83 us -> 3.97 us
    all_to_all x1 -> x0, blocking collectives: 21.3 us -> none  [exchange(): lax.all_to_all(rows.reshape(-1), AXES, 0, 0, tiled=True).reshape(rows.shape)]
    all_to_all x1 -> x2, waiting for transfers between devices: 0.01 us -> 10.1 us  [exchange(): lax.all_to_all(rows.reshape(-1), AXES, 0, 0, tiled=True).reshape(rows.shape)]
    all_to_all x1 -> x2, starting transfers between devices: 11.5 us -> 18 us  [exchange(): lax.all_to_all(rows.reshape(-1), AXES, 0, 0, tiled=True).reshape(rows.shape)]
    pallas_call x1, Pallas kernels: 12.6 us -> 8.28 us  [local(): pl.pallas_call(field_kernel, out_shape=shape(DEVICES, 128), scratch_shape...]
    ppermute x2, starting transfers between devices: 5.82 us -> 9.65 us  [shifted(): return lax.ppermute(value, AXES, pairs)]
    pallas_call x1 -> x3, Pallas kernels: 7.64 us -> 4.54 us  [the longest x1 2.82 us: local(): pl.pallas_call(density_kernel, out_shape=shape(3 * LPTS, LANES), in_specs...]
    sub x2 -> x0, other arithmetic: 1.93 us -> none  [the longest x1 1.23 us: local(): leaf_parent - 2 * (device - 1)]
    pallas_call x1, Pallas kernels: 3.2 us -> 1.53 us  [local(): pl.pallas_call(fiber_kernel, out_shape=shape(8, 256), scratch_shapes=[plt...]
  transfers between devices with their start and end apart: 3 -> 4, of which waited for: 1 -> 2; matrix products, arithmetic and copies ran while one was open for 6% -> 0% of each run, Pallas kernels for 11% -> 8%
where the time goes in v1:
time: 59.4 us; the launch traced here: 59 us
  starting transfers between devices  27.7 us (47%)
  Pallas kernels  17.1 us (29%)
  waiting for transfers between devices  10.1 us (17%)
  local copies, waits for them, and re-layouts  3.97 us (7%)
    all_to_all x2, starting transfers between devices, exchange(): lax.all_to_all(rows.reshape(-1), AXES, 0, 0, tiled=True).reshape(rows.shape)  18 us
    all_to_all x2, waiting for transfers between devices, exchange(): lax.all_to_all(rows.reshape(-1), AXES, 0, 0, tiled=True).reshape(rows.shape)  10.1 us
    ppermute x2, starting transfers between devices, shifted(): return lax.ppermute(value, AXES, pairs)  9.65 us
    pallas_call x1, Pallas kernels, local(): pl.pallas_call(field_kernel, out_shape=shape(DEVICES, 128), scratch_shape...  8.28 us
    unnamed x22, local copies, waits for them, and re-layouts  3.97 us
    pallas_call x1, Pallas kernels, local(): pl.pallas_call(density_kernel, out_shape=shape(3 * LPTS, LANES), in_specs...  2.82 us
    pallas_call x1, Pallas kernels, local(): pl.pallas_call(pack_kernel, out_shape=(shape(CHUNKS * 128, 128), shape(1,...  2.7 us
    pallas_call x2, Pallas kernels, split_up(): pl.pallas_call(split_kernel, grid=(count // step,), out_shape=jax.ShapeDt...  1.72 us
  transfers between devices with their start and end apart: 4, of which 2 were waited for; matrix products, arithmetic and copies ran while one was open for 0% of the time, Pallas kernels for 8%

profile of v1, /device:TPU:1, one launch (start us, length us, event | category | flops | bytes accessed | tf_op | source)
XLA Modules:
  0.0 59.0 jit_solution(3235345737801883355)
XLA Ops:
  0.0 2.7 %pack.1 = (f32[1920,128]{1,0:T(8,128)}, f32[1,512]{1,0:T(1,128)}) custom-call(f32[3,512]{1,0:T(4,128)} %pos_ref.1, f32[3,512]{1,0:T(4,128)} %force_ref.1, s32[1,512]{1,0:T(1,128)} %bitcast.16), custom_call_target="tpu_custom_call" | custom-call | flops 100000000 | bytes 1000000 | tf_op jit(solution)/shard_map/pack/pallas_call | solution.py:364
  2.7 0.0 copy-start.8
  2.7 11.5 %all-to-all-start = ((f32[128,1920,1]{1,2,0:T(1,128)}), f32[128,1920,1]{1,2,0:T(1,128)S(1)}, u32[]{:S(2)}, u32[]{:S(2)}) async-start(f32[128,1920,1]{1,2,0:T(1,128)} %bitcast.19), calls=%async_computation | async-start | bytes 1966080 | tf_op jit(solution)/shard_map/all_to_all | solution.py:354
  14.2 3.3 %collective-permute-start = (f32[3,2,128]{2,1,0:T(2,128)}, f32[3,2,128]{2,1,0:T(2,128)S(1)}, u32[]{:S(2)}, u32[]{:S(2)}) collective-permute-start(f32[3,2,128]{2,1,0:T(2,128)} %bitcast.13), channel_id=1, source_target_pairs={{0,1},{1,2},{2,3},{3,4},{4,5},{5,6},{6,7},{7,8},{8,9},{9,10},{10,1... | collective-permute-start | bytes 9224 | tf_op jit(solution)/shard_map/ppermute | solution.py:346
  17.5 6.4 %collective-permute-start.1 = (f32[3,2,128]{2,1,0:T(2,128)}, f32[3,2,128]{2,1,0:T(2,128)S(1)}, u32[]{:S(2)}, u32[]{:S(2)}) collective-permute-start(f32[3,2,128]{2,1,0:T(2,128)} %bitcast.14), channel_id=1, source_target_pairs={{1,0},{2,1},{3,2},{4,3},{5,4},{6,5},{7,6},{8,7},{9,8},{10,9},{11,1... | collective-permute-start | bytes 9224 | tf_op jit(solution)/shard_map/ppermute | solution.py:346
  23.9 0.0 copy-start
  23.9 2.3 %copy-done = f32[8,384,384]{2,1,0:T(8,128)S(1)} copy-done((f32[8,384,384]{2,1,0:T(8,128)S(1)}, f32[8,384,384]{2,1,0:T(8,128)}, u32[]{:S(2)}) %copy-start) | copy-done | bytes 4718616
  26.2 1.2 %split.2.maps_ref = bf16[2,8,384,384]{3,2,1,0:T(8,128)(2,1)S(1)} custom-call(f32[8,384,384]{2,1,0:T(8,128)S(1)} %copy-done), custom_call_target="tpu_custom_call" | custom-call | flops 4718592 | bytes 9437184 | tf_op jit(solution)/shard_map/split/pallas_call | solution.py:330
  27.4 0.0 copy-start.9
  27.4 0.0 copy-start.10
  27.4 0.0 collective-permute-done.before_ref
  27.5 0.0 collective-permute-done.1.after_ref
  27.5 0.0 copy-done.2
  27.5 0.0 copy-done.3
  27.5 0.0 copy-done.7
  27.5 0.0 copy-done.8
  27.5 2.8 %density.1.density_ref = f32[96,512]{1,0:T(8,128)S(1)} custom-call(s32[16]{0:T(128)S(1)} %copy-done.7, s32[16]{0:T(128)S(1)} %copy-done.8, f32[3,2,128]{2,1,0:T(2,128)S(1)} %collective-permute-done.before_ref, f32[3,2,128]{2,1,0:T(2,128)S(1)} %bitcast.15, f32[3,2,128]{2,1,0:T(2,128)S(1)} %collective-permute-done.1.after_ref, f32[3,16,128]{2,1,0:T(8,128)S(1)} %bitcast.12, ...), custom_call_target="tpu_custom_call" | custom-call | flops 1000000000 | bytes 5000000 | tf_op jit(solution)/shard_map/density/pallas_call | solution.py:378
  30.3 0.0 copy-start.4
  30.3 0.0 copy-start.5
  30.4 0.0 copy-start.6
  30.4 2.4 %all-to-all-done = f32[128,1920,1]{1,2,0:T(1,128)S(1)} async-done(((f32[128,1920,1]{1,2,0:T(1,128)}), f32[128,1920,1]{1,2,0:T(1,128)S(1)}, u32[]{:S(2)}, u32[]{:S(2)}) %all-to-all-start) | async-done | bytes 983072 | tf_op jit(solution)/shard_map/all_to_all | solution.py:354
  32.8 0.0 copy-done.9
  32.8 0.0 copy-done.10
  32.8 8.3 %field.1 = f32[128,128]{1,0:T(8,128)} custom-call(f32[1920,128]{1,0:T(8,128)S(1)} %bitcast.10, s32[16,27]{1,0:T(8,128)S(1)} %copy-done.9, f32[96,512]{1,0:T(8,128)S(1)} %density.1.density_ref, f32[96,512]{1,0:T(8,128)S(1)} %copy-done.10), custom_call_target="tpu_custom_call" | custom-call | flops 1000000000 | bytes 2000000 | tf_op jit(solution)/shard_map/field/pallas_call | solution.py:393
  41.1 6.5 %all-to-all-start.1 = ((f32[128,128,1]{1,2,0:T(1,128)}), f32[128,128,1]{1,2,0:T(1,128)S(1)}, u32[]{:S(2)}, u32[]{:S(2)}) async-start(f32[128,128,1]{1,2,0:T(1,128)} %bitcast.6), calls=%async_computation.1 | async-start | bytes 131072 | tf_op jit(solution)/shard_map/all_to_all | solution.py:354
  47.6 0.0 copy-start.1
  47.6 1.6 %copy-done.1 = f32[8,256,256]{2,1,0:T(8,128)S(1)} copy-done((f32[8,256,256]{2,1,0:T(8,128)S(1)}, f32[8,256,256]{2,1,0:T(8,128)}, u32[]{:S(2)}) %copy-start.1) | copy-done | bytes 2097176
  49.2 0.5 split.3.blocks_ref
  49.8 7.7 %all-to-all-done.1 = f32[128,128,1]{1,2,0:T(1,128)S(1)} async-done(((f32[128,128,1]{1,2,0:T(1,128)}), f32[128,128,1]{1,2,0:T(1,128)S(1)}, u32[]{:S(2)}, u32[]{:S(2)}) %all-to-all-start.1) | async-done | bytes 65568 | tf_op jit(solution)/shard_map/all_to_all | solution.py:354
  57.4 0.0 copy-done.4
  57.4 0.0 copy-done.5
  57.4 1.5 %fiber.1 = f32[8,256]{1,0:T(8,128)} custom-call(f32[128,128]{1,0:T(8,128)S(1)} %bitcast.11, s32[1,512]{1,0:T(1,128)S(1)} %bitcast.17, f32[1,512]{1,0:T(1,128)S(1)} %copy-done.6, f32[1,512]{1,0:T(1,128)S(1)} %bitcast.18, bf16[2,8,256,256]{3,2,1,0:T(8,128)(2,1)S(1)} %split.3.blocks_ref), custom_call_target="tpu_custom_call" | custom-call | flops 100000000 | bytes 2000000 | tf_op jit(solution)/shard_map/fiber/pallas_call | solution.py:409
  (4 shorter events, 0.0 us)
Async XLA Ops:
  2.7 24.8 %copy-start.2 = (f32[16,3,128]{2,0,1:T(8,128)S(1)}, f32[16,3,128]{2,0,1:T(8,128)}, u32[]{:S(2)}) copy-start(f32[16,3,128]{2,0,1:T(8,128)} %param.16) | copy-start | bytes 73732
  2.7 24.8 %copy-start.3 = (f32[2,3,128]{2,0,1:T(2,128)S(1)}, f32[2,3,128]{2,0,1:T(2,128)}, u32[]{:S(2)}) copy-start(f32[2,3,128]{2,0,1:T(2,128)} %param.17) | copy-start | bytes 9220
  2.7 24.8 %copy-start.7 = (s32[16]{0:T(128)S(1)}, s32[16]{0:T(128)}, u32[]{:S(2)}) copy-start(s32[16]{0:T(128)} %parent_ref.1) | copy-start | bytes 196
  2.7 24.8 %copy-start.8 = (s32[16]{0:T(128)S(1)}, s32[16]{0:T(128)}, u32[]{:S(2)}) copy-start(s32[16]{0:T(128)} %octant_ref.1) | copy-start | bytes 196
  2.7 30.1 %all-to-all-start = ((f32[128,1920,1]{1,2,0:T(1,128)}), f32[128,1920,1]{1,2,0:T(1,128)S(1)}, u32[]{:S(2)}, u32[]{:S(2)}) async-start(f32[128,1920,1]{1,2,0:T(1,128)} %bitcast.19), calls=%async_computation | async-start | bytes 1966080 | tf_op jit(solution)/shard_map/all_to_all | solution.py:354
  14.2 13.2 %collective-permute-start = (f32[3,2,128]{2,1,0:T(2,128)}, f32[3,2,128]{2,1,0:T(2,128)S(1)}, u32[]{:S(2)}, u32[]{:S(2)}) collective-permute-start(f32[3,2,128]{2,1,0:T(2,128)} %bitcast.13), channel_id=1, source_target_pairs={{0,1},{1,2},{2,3},{3,4},{4,5},{5,6},{6,7},{7,8},{8,9},{9,10},{10,1... | collective-permute-start | bytes 9224 | tf_op jit(solution)/shard_map/ppermute | solution.py:346
  17.5 10.0 %collective-permute-start.1 = (f32[3,2,128]{2,1,0:T(2,128)}, f32[3,2,128]{2,1,0:T(2,128)S(1)}, u32[]{:S(2)}, u32[]{:S(2)}) collective-permute-start(f32[3,2,128]{2,1,0:T(2,128)} %bitcast.14), channel_id=1, source_target_pairs={{1,0},{2,1},{3,2},{4,3},{5,4},{6,5},{7,6},{8,7},{9,8},{10,9},{11,1... | collective-permute-start | bytes 9224 | tf_op jit(solution)/shard_map/ppermute | solution.py:346
  23.9 2.3 %copy-start = (f32[8,384,384]{2,1,0:T(8,128)S(1)}, f32[8,384,384]{2,1,0:T(8,128)}, u32[]{:S(2)}) copy-start(f32[8,384,384]{2,1,0:T(8,128)} %blocks_ref.2) | copy-start | bytes 14155780
  27.4 5.4 %copy-start.9 = (s32[16,27]{1,0:T(8,128)S(1)}, s32[16,27]{1,0:T(8,128)}, u32[]{:S(2)}) copy-start(s32[16,27]{1,0:T(8,128)} %near_ref.1) | copy-start | bytes 5188
  27.4 5.4 %copy-start.10 = (f32[96,512]{1,0:T(8,128)S(1)}, f32[96,512]{1,0:T(8,128)}, u32[]{:S(2)}) copy-start(f32[96,512]{1,0:T(8,128)} %constant.2.clone.shell_ref) | copy-start | bytes 589828
  30.3 27.1 %copy-start.4 = (s32[512]{0:T(512)S(1)}, s32[512]{0:T(512)}, u32[]{:S(2)}) copy-start(s32[512]{0:T(512)} %param.15) | copy-start | bytes 6148
  30.3 27.1 %copy-start.5 = (f32[512]{0:T(512)S(1)}, f32[512]{0:T(512)}, u32[]{:S(2)}) copy-start(f32[512]{0:T(512)} %param.14) | copy-start | bytes 6148
  30.4 27.1 %copy-start.6 = (f32[1,512]{1,0:T(1,128)S(1)}, f32[1,512]{1,0:T(1,128)}, u32[]{:S(2)}) copy-start(f32[1,512]{1,0:T(1,128)} %get-tuple-element.12.rank_ref) | copy-start | bytes 6148
  41.1 16.3 %all-to-all-start.1 = ((f32[128,128,1]{1,2,0:T(1,128)}), f32[128,128,1]{1,2,0:T(1,128)S(1)}, u32[]{:S(2)}, u32[]{:S(2)}) async-start(f32[128,128,1]{1,2,0:T(1,128)} %bitcast.6), calls=%async_computation.1 | async-start | bytes 131072 | tf_op jit(solution)/shard_map/all_to_all | solution.py:354
  47.6 1.6 %copy-start.1 = (f32[8,256,256]{2,1,0:T(8,128)S(1)}, f32[8,256,256]{2,1,0:T(8,128)}, u32[]{:S(2)}) copy-start(f32[8,256,256]{2,1,0:T(8,128)} %blocks_ref.3) | copy-start | bytes 6291460

commit v2 on v1

--- a/solution.py
+++ b/solution.py
@@ -16,9 +16,10 @@
 NEAR = 27
 NEQ = 128
 LANES = LEAVES * LPTS
+GROUPS = NEQ // LPTS
+FAR = GROUPS * LEAVES
 WORDS = 7 * SPAN * CAP
 CHUNKS = 15
-MAPS_GRANT = 8
 EPS2 = 0.05**2
 MARGIN = 0.05
 SHELL = 2.95
@@ -62,10 +63,20 @@
     angle = (q * np.float32(GOLDEN)).astype(np.float32)
     w = np.stack([radius * np.cos(angle), radius * np.sin(angle), h]).astype(np.float32)
     s = w / np.max(np.abs(w), axis=0, keepdims=True)
-    table = np.zeros((3, LPTS, LANES), np.float32)
-    for g in range(NEQ // LPTS):
-        table[:, :, NEAR + g :: LPTS] = s[:, g * LPTS : (g + 1) * LPTS, None]
-    return table.reshape(3 * LPTS, LANES)
+    table = np.zeros((3, LPTS, 128), np.float32)
+    for g in range(GROUPS):
+        table[:, :, g * LEAVES : (g + 1) * LEAVES] = s[:, g * LPTS : (g + 1) * LPTS, None]
+    return table.reshape(3 * LPTS, 128)
+
+
+def lane_place():
+    lane = iota((1, LANES), 1)
+    near = lane - FAR
+    leaf = ((near.astype(F32) + 0.5) * (1.0 / NEAR)).astype(jnp.int32)
+    place = near - leaf * NEAR
+    is_near = (lane >= FAR) & (lane < FAR + LEAVES * NEAR)
+    leaf = jnp.where(lane < FAR, lane & (LEAVES - 1), jnp.where(is_near, leaf, 0))
+    return leaf, jnp.where(is_near, place, -1)
 
 
 def device_index():
@@ -101,6 +112,31 @@
         message_ref[pl.ds(i, DEVICES, stride=CHUNKS), :] = rows_ref[i * 128 : (i + 1) * 128, :].T
 
 
+def prepare_kernel(near_ref, maps_ref, split_ref, near_hot_ref, own_hot_ref, rows_ref):
+    step = pl.program_id(0)
+
+    @pl.when(step == 0)
+    def _():
+        leaf, place = lane_place()
+        near = near_ref[...] - LEAVES * (device_index() - REACH)
+        spread = (iota((NEAR, LANES), 0) == place).astype(F32).astype(BF16)
+        own = iota((LEAVES, LANES), 0) == leaf
+        values = jnp.concatenate([near & 3, near >> 2], axis=0).astype(F32).astype(BF16)
+        values = dot(values, spread, NN)
+        for k in range(2):
+            value = jnp.where(own, values[k * LEAVES : (k + 1) * LEAVES], 0.0)
+            value = jnp.sum(value, axis=0, keepdims=True).astype(jnp.int32)
+            rows_ref[k : k + 1, :] = jnp.where(place >= 0, value, -1)
+        rows_ref[2:3, :] = leaf & 3
+        rows_ref[3:4, :] = (leaf + REACH * LEAVES) >> 2
+
+    split_ref[0], split_ref[1] = two(maps_ref[...])
+    leaf_row = iota((128, LANES), 0)
+    for k, ref in enumerate((near_hot_ref, own_hot_ref)):
+        row = jnp.where(rows_ref[2 * k : 2 * k + 1, :] == step, rows_ref[2 * k + 1 : 2 * k + 2, :], -1)
+        ref[...] = (leaf_row == row).astype(F32).astype(BF16)
+
+
 def density_kernel(
     parent_ref, octant_ref, before_ref, own_ref, after_ref, local_ref, maps_ref, out_ref,
     six_ref, picked_ref,
@@ -110,39 +146,36 @@
         source = (before_ref, own_ref, after_ref)[j // 2]
         for c in range(3):
             six_ref[c * 8 + j : c * 8 + j + 1, :] = source[c, j % 2 : j % 2 + 1, :]
+    lane = iota((1, 128), 1) % LEAVES
+    octants = jnp.zeros((1, 128), jnp.int32)
     for l in range(LEAVES):
+        octants = jnp.where(lane == l, octant_ref[l], octants)
         for c in range(3):
             picked_ref[l : l + 1, c * NEQ : (c + 1) * NEQ] = six_ref[
                 pl.ds(c * 8 + parent_ref[l] - first_parent, 1), :
             ]
-    lane = iota((1, 2 * LEAVES), 1) % LEAVES
-    octants = jnp.zeros((1, 2 * LEAVES), jnp.int32)
-    for l in range(LEAVES):
-        octants = jnp.where(lane == l, octant_ref[l], octants)
-    weights = jnp.concatenate(two(picked_ref[...]), axis=0)
-    total = jnp.zeros((3 * NEQ, 2 * LEAVES), F32)
+    high, low = two(picked_ref[...])
+    weights = jnp.concatenate([high] * GROUPS + [low] * GROUPS, axis=0)
+    total = jnp.zeros((3 * NEQ, 128), F32)
     for o in range(8):
         image = dot(maps_ref[0, o], weights, NT) + dot(maps_ref[1, o], weights, NT)
         total = jnp.where(octants == o, image, total)
-    moved = total[:, :LEAVES] + total[:, LEAVES:]
-    lane = iota((LEAVES, LANES), 1)
-    row = iota((LEAVES, LANES), 0)
-    pieces = []
+    group = iota((1, 128), 1) // LEAVES
+    nothing = jnp.zeros((NEQ - FAR, NEQ), F32)
     for c in range(3):
-        own = jnp.concatenate([local_ref[c], jnp.zeros((NEQ - LEAVES, NEQ), F32)], axis=0).T
-        pieces.append(own[:, :LEAVES] + moved[c * NEQ : (c + 1) * NEQ])
-    placed = jnp.zeros((3 * LPTS, LANES), F32)
-    for g in range(NEQ // LPTS):
-        group = jnp.concatenate([p[g * LPTS : (g + 1) * LPTS] for p in pieces], axis=0)
-        place = (lane == row * LPTS + NEAR + g).astype(F32)
-        placed = placed + lax.dot_general(
-            group, place, NN, precision=HIGHEST, preferred_element_type=F32
-        )
-    out_ref[...] = placed
+        local = jnp.concatenate([local_ref[c]] * GROUPS + [nothing], axis=0).T
+        moved = total[c * NEQ : (c + 1) * NEQ]
+        placed = jnp.zeros((LPTS, 128), F32)
+        for g in range(GROUPS):
+            rows = slice(g * LPTS, (g + 1) * LPTS)
+            here = group % GROUPS == g
+            placed = jnp.where(here, moved[rows] + local[rows], placed)
+        placed = placed + pltpu.roll(placed, 128 - FAR, 1)
+        out_ref[c * LPTS : (c + 1) * LPTS, :] = jnp.where(group < GROUPS, placed, 0.0)
 
 
 def field_kernel(
-    arrived_ref, near_ref, density_ref, shell_ref, out_ref,
+    arrived_ref, near_hot_ref, own_hot_ref, density_ref, shell_ref, out_ref,
     turned_ref, tree_ref, source_ref, target_ref, partial_ref, back_ref,
 ):
     entries = SPAN * CAP
@@ -185,31 +218,8 @@
             )
     everything = jnp.concatenate([t for s in range(3) for t in terms[s]], axis=0)
     positions = jnp.concatenate([t for s in range(3) for t in terms[s][:3]], axis=0)
-    leaf_row = iota((128, LANES), 0)
-
-    def hot(quarter, row):
-        return jnp.concatenate(
-            [
-                (leaf_row == jnp.where(quarter == w, row, -1)).astype(F32).astype(BF16)
-                for w in range(4)
-            ],
-            axis=0,
-        )
-
-    lane = iota((1, LANES), 1)
-    spot = lane % LPTS
-    near = near_ref[...] - LEAVES * (device_index() - REACH)
-    spread = (iota((NEAR, LANES), 0) == spot).astype(F32).astype(BF16)
-    own = iota((LEAVES, LANES), 0) == lane // LPTS
-
-    def as_lanes(value):
-        value = dot(value.astype(F32).astype(BF16), spread, NN)
-        return jnp.sum(jnp.where(own, value, 0.0), axis=0, keepdims=True).astype(jnp.int32)
-
-    near_row = jnp.where(spot < NEAR, as_lanes(near >> 2), -1)
-    leaf = lane // LPTS + REACH * LEAVES
-    gathered = thirds(dot(everything, hot(as_lanes(near & 3), near_row), NN), 6 * LPTS)
-    targets = thirds(dot(positions, hot(leaf & 3, leaf >> 2), NN), 3 * LPTS)
+    gathered = thirds(dot(everything, near_hot_ref[...], NN), 6 * LPTS)
+    targets = thirds(dot(positions, own_hot_ref[...], NN), 3 * LPTS)
     for k in range(LANES // 128):
         target_ref[k * 96 : (k + 1) * 96, :] = targets[:, k * 128 : (k + 1) * 128]
     axes = [targets[c * LPTS : (c + 1) * LPTS] for c in range(3)]
@@ -221,14 +231,15 @@
         ),
         jnp.max(jnp.abs(axes[2] - centers[2]), axis=0, keepdims=True),
     ) + MARGIN
-    far = (spot >= NEAR) & (spot < NEAR + NEQ // LPTS)
     for c in range(3):
         rows = slice(c * LPTS, (c + 1) * LPTS)
-        shell = jnp.where(far, centers[c], 0.0) + (SHELL * half) * shell_ref[rows, :]
-        source_ref[rows, :] = gathered[rows, :] + shell
-    source_ref[3 * LPTS :, :] = gathered[3 * LPTS :, :] + density_ref[...]
-
-    soft = jnp.where(far, 0.0, EPS2)
+        more = slice((3 + c) * LPTS, (4 + c) * LPTS)
+        first = gathered[rows, :128] + (SHELL * half[:, :128]) * shell_ref[rows, :]
+        source_ref[rows, :128] = first + jnp.where(iota((1, 128), 1) < FAR, centers[c][:, :128], 0.0)
+        source_ref[rows, 128:] = gathered[rows, 128:]
+        source_ref[more, :128] = gathered[more, :128] + density_ref[rows, :]
+        source_ref[more, 128:] = gathered[more, 128:]
+    soft = jnp.where(iota((1, LANES), 1) < FAR, 0.0, EPS2)
     for chunk in range(LANES // 128):
         lanes = slice(chunk * 128, (chunk + 1) * 128)
         soft_c = soft[:, lanes]
@@ -254,15 +265,11 @@
 
         lax.fori_loop(0, LPTS, step, 0, unroll=8)
 
-    same = (iota((LEAVES, LANES), 1) // LPTS == iota((LEAVES, LANES), 0)).astype(F32)
+    same = (iota((LEAVES, LANES), 0) == lane_place()[0]).astype(F32).astype(BF16)
+    same = jnp.concatenate([same] * 3, axis=1)
     partial = jnp.concatenate([partial_ref[k * 96 : (k + 1) * 96, :] for k in range(4)], axis=1)
-    by_leaf = [
-        lax.dot_general(
-            same, partial[c * LPTS : (c + 1) * LPTS, :], NT, precision=HIGHEST,
-            preferred_element_type=F32,
-        )
-        for c in range(3)
-    ]
+    partial = jnp.concatenate(three(partial), axis=1).astype(BF16)
+    by_leaf = [dot(same, partial[c * LPTS : (c + 1) * LPTS, :], NT) for c in range(3)]
     velocity = jnp.concatenate(by_leaf, axis=0) * (1.0 / EIGHT_PI)
     velocity = jnp.concatenate(three(velocity), axis=0).astype(BF16)
     node_row = iota((LPTS, DEVICES), 0)
@@ -286,7 +293,8 @@
 
 
 def split_kernel(blocks_ref, out_ref):
-    out_ref[0], out_ref[1] = two(blocks_ref[...])
+    for i in range(2):
+        out_ref[0, i], out_ref[1, i] = two(blocks_ref[i].T)
 
 
 def fiber_kernel(
@@ -315,30 +323,13 @@
     row = iota((16, 256), 0) % 8
     total = jnp.zeros((16, 256), F32)
     for i in range(8):
-        image = dot(vector, blocks_ref[0, i], NT) + dot(vector, blocks_ref[1, i], NT)
+        image = dot(vector, blocks_ref[0, i], NN) + dot(vector, blocks_ref[1, i], NN)
         total = jnp.where(row == i, image, total)
     out_ref[...] = total[:8] + total[8:]
 
 
 def shape(*dims):
     return jax.ShapeDtypeStruct(dims, F32)
-
-
-def split_up(value, step, mib):
-    count, *rest = value.shape
-    zeros = (0,) * len(rest)
-    return pl.pallas_call(
-        split_kernel,
-        grid=(count // step,),
-        out_shape=jax.ShapeDtypeStruct((2, count, *rest), BF16),
-        in_specs=[pl.BlockSpec((step, *rest), lambda i: (i, *zeros))],
-        out_specs=pl.BlockSpec((2, step, *rest), lambda i: (0, i, *zeros)),
-        cost_estimate=pl.CostEstimate(
-            flops=4 * value.size, bytes_accessed=8 * value.size, transcendentals=0
-        ),
-        compiler_params=grant(mib),
-        name="split",
-    )(value)
 
 
 def shifted(value, by):
@@ -375,9 +366,41 @@
 
     vmem = pl.BlockSpec(memory_space=pltpu.VMEM)
     smem = pl.BlockSpec(memory_space=pltpu.SMEM)
+    maps, near_hot, own_hot = pl.pallas_call(
+        prepare_kernel,
+        grid=(4,),
+        out_shape=(
+            jax.ShapeDtypeStruct((2, 8, 384, 384), BF16),
+            jax.ShapeDtypeStruct((LANES, LANES), BF16),
+            jax.ShapeDtypeStruct((LANES, LANES), BF16),
+        ),
+        in_specs=[
+            pl.BlockSpec((LEAVES, NEAR), lambda i: (0, 0)),
+            pl.BlockSpec((2, 384, 384), lambda i: (i, 0, 0)),
+        ],
+        out_specs=(
+            pl.BlockSpec((2, 2, 384, 384), lambda i: (0, i, 0, 0)),
+            pl.BlockSpec((128, LANES), lambda i: (i, 0)),
+            pl.BlockSpec((128, LANES), lambda i: (i, 0)),
+        ),
+        scratch_shapes=[pltpu.VMEM((8, LANES), jnp.int32)],
+        cost_estimate=pl.CostEstimate(flops=5 * 10**6, bytes_accessed=10**7, transcendentals=0),
+        compiler_params=grant(8),
+        name="prepare",
+    )(near_list, l2l_maps)
+    split = pl.pallas_call(
+        split_kernel,
+        grid=(4,),
+        out_shape=jax.ShapeDtypeStruct((2, 8, 256, 256), BF16),
+        in_specs=[pl.BlockSpec((2, 256, 256), lambda i: (i, 0, 0))],
+        out_specs=pl.BlockSpec((2, 2, 256, 256), lambda i: (0, i, 0, 0)),
+        cost_estimate=pl.CostEstimate(flops=2 * 10**6, bytes_accessed=4 * 10**6, transcendentals=0),
+        compiler_params=grant(4),
+        name="split",
+    )(blocks)
     density = pl.pallas_call(
         density_kernel,
-        out_shape=shape(3 * LPTS, LANES),
+        out_shape=shape(3 * LPTS, 128),
         in_specs=[smem, smem, vmem, vmem, vmem, vmem, vmem],
         scratch_shapes=[
             pltpu.VMEM((24, NEQ), F32),
@@ -388,7 +411,7 @@
         name="density",
     )(
         leaf_parent, leaf_octant, from_before, parent_local, from_after,
-        leaf_local, split_up(l2l_maps, 2, MAPS_GRANT),
+        leaf_local, maps,
     )
     back = pl.pallas_call(
         field_kernel,
@@ -404,7 +427,7 @@
         cost_estimate=pl.CostEstimate(flops=10**9, bytes_accessed=2 * 10**6, transcendentals=0),
         compiler_params=grant(16),
         name="field",
-    )(arrived, near_list, density, jnp.asarray(shell_table()))
+    )(arrived, near_hot, own_hot, density, jnp.asarray(shell_table()))
     returned = exchange(back)
     return pl.pallas_call(
         fiber_kernel,
@@ -413,7 +436,7 @@
         cost_estimate=pl.CostEstimate(flops=10**8, bytes_accessed=2 * 10**6, transcendentals=0),
         compiler_params=grant(8),
         name="fiber",
-    )(returned, slot, rank, tension.reshape(1, NODES), split_up(blocks, 2, 4))
+    )(returned, slot, rank, tension.reshape(1, NODES), split)
 
 
 def solution(mesh):

time: 59.4 us -> 58.3 us (0.981)
  starting transfers between devices: 27.7 us -> 26.9 us
  waiting for transfers between devices: 10.1 us -> 9.36 us
  local copies, waits for them, and re-layouts: 3.97 us -> 4.65 us
    all_to_all x2, starting transfers between devices: 18 us -> 17.3 us  [exchange(): lax.all_to_all(rows.reshape(-1), AXES, 0, 0, tiled=True).reshape(rows.shape)]
    all_to_all x2, waiting for transfers between devices: 10.1 us -> 9.35 us  [exchange(): lax.all_to_all(rows.reshape(-1), AXES, 0, 0, tiled=True).reshape(rows.shape)]
    unnamed x22, local copies, waits for them, and re-layouts: 3.97 us -> 4.65 us
where the time goes in v2:
time: 58.3 us; the launch traced here: 57.9 us
  starting transfers between devices  26.9 us (46%)
  Pallas kernels  16.8 us (29%)
  waiting for transfers between devices  9.36 us (16%)
  local copies, waits for them, and re-layouts  4.65 us (8%)
    all_to_all x2, starting transfers between devices, exchange(): lax.all_to_all(rows.reshape(-1), AXES, 0, 0, tiled=True).reshape(rows.shape)  17.3 us
    ppermute x2, starting transfers between devices, shifted(): return lax.ppermute(value, AXES, pairs)  9.65 us
    all_to_all x2, waiting for transfers between devices, exchange(): lax.all_to_all(rows.reshape(-1), AXES, 0, 0, tiled=True).reshape(rows.shape)  9.35 us
    pallas_call x1, Pallas kernels, local(): pl.pallas_call(field_kernel, out_shape=shape(DEVICES, 128), scratch_shape...  8.1 us
    unnamed x22, local copies, waits for them, and re-layouts  4.65 us
    pallas_call x1, Pallas kernels, local(): pl.pallas_call(pack_kernel, out_shape=(shape(CHUNKS * 128, 128), shape(1,...  2.75 us
    pallas_call x1, Pallas kernels, local(): pl.pallas_call(density_kernel, out_shape=shape(3 * LPTS, 128), in_specs=[...  2.1 us
    pallas_call x1, Pallas kernels, local(): pl.pallas_call(prepare_kernel, grid=(4,), out_shape=(jax.ShapeDtypeStruct...  1.53 us
  transfers between devices with their start and end apart: 4, of which 2 were waited for; matrix products, arithmetic and copies ran while one was open for 0% of the time, Pallas kernels for 8%

profile of v2, /device:TPU:1, one launch (start us, length us, event | category | flops | bytes accessed | tf_op | source)
XLA Modules:
  0.0 57.9 jit_solution(4552961121595407525)
XLA Ops:
  0.0 0.0 copy-start.4
  0.0 0.0 copy-start.2
  0.0 2.8 %pack.1 = (f32[1920,128]{1,0:T(8,128)}, f32[1,512]{1,0:T(1,128)}) custom-call(f32[3,512]{1,0:T(4,128)} %pos_ref.1, f32[3,512]{1,0:T(4,128)} %force_ref.1, s32[1,512]{1,0:T(1,128)} %bitcast.16), custom_call_target="tpu_custom_call" | custom-call | flops 100000000 | bytes 1000000 | tf_op jit(solution)/shard_map/pack/pallas_call | solution.py:355
  2.8 11.5 %all-to-all-start = ((f32[128,1920,1]{1,2,0:T(1,128)}), f32[128,1920,1]{1,2,0:T(1,128)S(1)}, u32[]{:S(2)}, u32[]{:S(2)}) async-start(f32[128,1920,1]{1,2,0:T(1,128)} %bitcast.19), calls=%async_computation | async-start | bytes 1966080 | tf_op jit(solution)/shard_map/all_to_all | solution.py:345
  14.3 3.3 %collective-permute-start = (f32[3,2,128]{2,1,0:T(2,128)}, f32[3,2,128]{2,1,0:T(2,128)S(1)}, u32[]{:S(2)}, u32[]{:S(2)}) collective-permute-start(f32[3,2,128]{2,1,0:T(2,128)} %bitcast.13), channel_id=1, source_target_pairs={{0,1},{1,2},{2,3},{3,4},{4,5},{5,6},{6,7},{7,8},{8,9},{9,10},{10,1... | collective-permute-start | bytes 9224 | tf_op jit(solution)/shard_map/ppermute | solution.py:337
  17.5 6.4 %collective-permute-start.1 = (f32[3,2,128]{2,1,0:T(2,128)}, f32[3,2,128]{2,1,0:T(2,128)S(1)}, u32[]{:S(2)}, u32[]{:S(2)}) collective-permute-start(f32[3,2,128]{2,1,0:T(2,128)} %bitcast.14), channel_id=1, source_target_pairs={{1,0},{2,1},{3,2},{4,3},{5,4},{6,5},{7,6},{8,7},{9,8},{10,9},{11,1... | collective-permute-start | bytes 9224 | tf_op jit(solution)/shard_map/ppermute | solution.py:337
  23.9 0.0 copy-start
  23.9 2.3 %copy-done = f32[8,384,384]{2,1,0:T(8,128)S(1)} copy-done((f32[8,384,384]{2,1,0:T(8,128)S(1)}, f32[8,384,384]{2,1,0:T(8,128)}, u32[]{:S(2)}) %copy-start) | copy-done | bytes 4718616
  26.3 0.7 %copy-done.3 = s32[16,27]{1,0:T(8,128)S(1)} copy-done((s32[16,27]{1,0:T(8,128)S(1)}, s32[16,27]{1,0:T(8,128)}, u32[]{:S(2)}) %copy-start.3) | copy-done | bytes 1752
  27.0 1.5 %prepare.1 = (bf16[2,8,384,384]{3,2,1,0:T(8,128)(2,1)S(1)}, bf16[512,512]{1,0:T(8,128)(2,1)S(1)}, bf16[512,512]{1,0:T(8,128)(2,1)S(1)}) custom-call(s32[16,27]{1,0:T(8,128)S(1)} %copy-done.3, f32[8,384,384]{2,1,0:T(8,128)S(1)} %copy-done), custom_call_target="tpu_custom_call" | custom-call | flops 5000000 | bytes 10000000 | tf_op jit(solution)/shard_map/prepare/pallas_call | solution.py:369
  28.5 0.0 collective-permute-done.before_ref
  28.5 0.0 collective-permute-done.1.after_ref
  28.5 0.0 copy-done.4
  28.5 0.0 copy-done.8
  28.6 0.0 copy-done.9
  28.6 0.0 copy-done.2
  28.6 2.1 %density.1.density_ref = f32[96,128]{1,0:T(8,128)S(1)} custom-call(s32[16]{0:T(128)S(1)} %copy-done.8, s32[16]{0:T(128)S(1)} %copy-done.9, f32[3,2,128]{2,1,0:T(2,128)S(1)} %collective-permute-done.before_ref, f32[3,2,128]{2,1,0:T(2,128)S(1)} %bitcast.15, f32[3,2,128]{2,1,0:T(2,128)S(1)} %collective-permute-done.1.after_ref, f32[3,16,128]{2,1,0:T(8,128)S(1)} %bitcast.12, ...), custom_call_target="tpu_custom_call" | custom-call | flops 1000000000 | bytes 5000000 | tf_op jit(solution)/shard_map/density/pallas_call | solution.py:401
  30.7 0.0 copy-start.5
  30.7 0.0 copy-start.6
  30.7 0.0 copy-start.7
  30.7 2.1 %all-to-all-done = f32[128,1920,1]{1,2,0:T(1,128)S(1)} async-done(((f32[128,1920,1]{1,2,0:T(1,128)}), f32[128,1920,1]{1,2,0:T(1,128)S(1)}, u32[]{:S(2)}, u32[]{:S(2)}) %all-to-all-start) | async-done | bytes 983072 | tf_op jit(solution)/shard_map/all_to_all | solution.py:345
  32.8 0.0 copy-done.10
  32.8 8.1 %field.1 = f32[128,128]{1,0:T(8,128)} custom-call(f32[1920,128]{1,0:T(8,128)S(1)} %bitcast.10, bf16[512,512]{1,0:T(8,128)(2,1)S(1)} %get-tuple-element.14.near_hot_ref, bf16[512,512]{1,0:T(8,128)(2,1)S(1)} %get-tuple-element.15.own_hot_ref, f32[96,128]{1,0:T(8,128)S(1)} %density.1.density_ref, f32[96,128]{1,0:T(8,128)S(1)} %copy-done.10), custom_call_target="tpu_custom_call" | custom-call | flops 1000000000 | bytes 2000000 | tf_op jit(solution)/shard_map/field/pallas_call | solution.py:416
  40.9 5.8 %all-to-all-start.1 = ((f32[128,128,1]{1,2,0:T(1,128)}), f32[128,128,1]{1,2,0:T(1,128)S(1)}, u32[]{:S(2)}, u32[]{:S(2)}) async-start(f32[128,128,1]{1,2,0:T(1,128)} %bitcast.6), calls=%async_computation.1 | async-start | bytes 131072 | tf_op jit(solution)/shard_map/all_to_all | solution.py:345
  46.8 0.0 copy-start.1
  46.8 1.6 %copy-done.1 = f32[8,256,256]{2,1,0:T(8,128)S(1)} copy-done((f32[8,256,256]{2,1,0:T(8,128)S(1)}, f32[8,256,256]{2,1,0:T(8,128)}, u32[]{:S(2)}) %copy-start.1) | copy-done | bytes 2097176
  48.4 1.0 %split.1.blocks_ref = bf16[2,8,256,256]{3,2,1,0:T(8,128)(2,1)S(1)} custom-call(f32[8,256,256]{2,1,0:T(8,128)S(1)} %copy-done.1), custom_call_target="tpu_custom_call" | custom-call | flops 2000000 | bytes 4000000 | tf_op jit(solution)/shard_map/split/pallas_call | solution.py:391
  49.4 7.2 %all-to-all-done.1 = f32[128,128,1]{1,2,0:T(1,128)S(1)} async-done(((f32[128,128,1]{1,2,0:T(1,128)}), f32[128,128,1]{1,2,0:T(1,128)S(1)}, u32[]{:S(2)}, u32[]{:S(2)}) %all-to-all-start.1) | async-done | bytes 65568 | tf_op jit(solution)/shard_map/all_to_all | solution.py:345
  56.6 0.0 copy-done.5
  56.6 0.0 copy-done.6
  56.6 0.0 copy-done.7
  56.6 1.3 %fiber.1 = f32[8,256]{1,0:T(8,128)} custom-call(f32[128,128]{1,0:T(8,128)S(1)} %bitcast.11, s32[1,512]{1,0:T(1,128)S(1)} %bitcast.17, f32[1,512]{1,0:T(1,128)S(1)} %copy-done.7, f32[1,512]{1,0:T(1,128)S(1)} %bitcast.18, bf16[2,8,256,256]{3,2,1,0:T(8,128)(2,1)S(1)} %split.1.blocks_ref), custom_call_target="tpu_custom_call" | custom-call | flops 100000000 | bytes 2000000 | tf_op jit(solution)/shard_map/fiber/pallas_call | solution.py:432
  (4 shorter events, 0.0 us)
Async XLA Ops:
  0.0 28.5 %copy-start.4 = (f32[2,3,128]{2,0,1:T(2,128)S(1)}, f32[2,3,128]{2,0,1:T(2,128)}, u32[]{:S(2)}) copy-start(f32[2,3,128]{2,0,1:T(2,128)} %param.17) | copy-start | bytes 9220
  0.0 28.5 %copy-start.8 = (s32[16]{0:T(128)S(1)}, s32[16]{0:T(128)}, u32[]{:S(2)}) copy-start(s32[16]{0:T(128)} %parent_ref.1) | copy-start | bytes 196
  0.0 28.5 %copy-start.9 = (s32[16]{0:T(128)S(1)}, s32[16]{0:T(128)}, u32[]{:S(2)}) copy-start(s32[16]{0:T(128)} %octant_ref.1) | copy-start | bytes 196
  0.0 28.6 %copy-start.2 = (f32[16,3,128]{2,0,1:T(8,128)S(1)}, f32[16,3,128]{2,0,1:T(8,128)}, u32[]{:S(2)}) copy-start(f32[16,3,128]{2,0,1:T(8,128)} %param.16) | copy-start | bytes 73732
  2.8 30.1 %copy-start.10 = (f32[96,128]{1,0:T(8,128)S(1)}, f32[96,128]{1,0:T(8,128)}, u32[]{:S(2)}) copy-start(f32[96,128]{1,0:T(8,128)} %constant.2.clone.shell_ref) | copy-start | bytes 147460
  2.8 30.1 %all-to-all-start = ((f32[128,1920,1]{1,2,0:T(1,128)}), f32[128,1920,1]{1,2,0:T(1,128)S(1)}, u32[]{:S(2)}, u32[]{:S(2)}) async-start(f32[128,1920,1]{1,2,0:T(1,128)} %bitcast.19), calls=%async_computation | async-start | bytes 1966080 | tf_op jit(solution)/shard_map/all_to_all | solution.py:345
  14.3 14.2 %collective-permute-start = (f32[3,2,128]{2,1,0:T(2,128)}, f32[3,2,128]{2,1,0:T(2,128)S(1)}, u32[]{:S(2)}, u32[]{:S(2)}) collective-permute-start(f32[3,2,128]{2,1,0:T(2,128)} %bitcast.13), channel_id=1, source_target_pairs={{0,1},{1,2},{2,3},{3,4},{4,5},{5,6},{6,7},{7,8},{8,9},{9,10},{10,1... | collective-permute-start | bytes 9224 | tf_op jit(solution)/shard_map/ppermute | solution.py:337
  17.5 11.0 %collective-permute-start.1 = (f32[3,2,128]{2,1,0:T(2,128)}, f32[3,2,128]{2,1,0:T(2,128)S(1)}, u32[]{:S(2)}, u32[]{:S(2)}) collective-permute-start(f32[3,2,128]{2,1,0:T(2,128)} %bitcast.14), channel_id=1, source_target_pairs={{1,0},{2,1},{3,2},{4,3},{5,4},{6,5},{7,6},{8,7},{9,8},{10,9},{11,1... | collective-permute-start | bytes 9224 | tf_op jit(solution)/shard_map/ppermute | solution.py:337
  23.9 2.3 %copy-start = (f32[8,384,384]{2,1,0:T(8,128)S(1)}, f32[8,384,384]{2,1,0:T(8,128)}, u32[]{:S(2)}) copy-start(f32[8,384,384]{2,1,0:T(8,128)} %maps_ref.1) | copy-start | bytes 14155780
  26.3 0.7 %copy-start.3 = (s32[16,27]{1,0:T(8,128)S(1)}, s32[16,27]{1,0:T(8,128)}, u32[]{:S(2)}) copy-start(s32[16,27]{1,0:T(8,128)} %near_ref.1) | copy-start | bytes 5188
  30.7 25.9 %copy-start.5 = (s32[512]{0:T(512)S(1)}, s32[512]{0:T(512)}, u32[]{:S(2)}) copy-start(s32[512]{0:T(512)} %param.15) | copy-start | bytes 6148
  30.7 25.9 %copy-start.6 = (f32[512]{0:T(512)S(1)}, f32[512]{0:T(512)}, u32[]{:S(2)}) copy-start(f32[512]{0:T(512)} %param.14) | copy-start | bytes 6148
  30.7 25.9 %copy-start.7 = (f32[1,512]{1,0:T(1,128)S(1)}, f32[1,512]{1,0:T(1,128)}, u32[]{:S(2)}) copy-start(f32[1,512]{1,0:T(1,128)} %get-tuple-element.18.rank_ref) | copy-start | bytes 6148
  40.9 15.6 %all-to-all-start.1 = ((f32[128,128,1]{1,2,0:T(1,128)}), f32[128,128,1]{1,2,0:T(1,128)S(1)}, u32[]{:S(2)}, u32[]{:S(2)}) async-start(f32[128,128,1]{1,2,0:T(1,128)} %bitcast.6), calls=%async_computation.1 | async-start | bytes 131072 | tf_op jit(solution)/shard_map/all_to_all | solution.py:345
  46.8 1.6 %copy-start.1 = (f32[8,256,256]{2,1,0:T(8,128)S(1)}, f32[8,256,256]{2,1,0:T(8,128)}, u32[]{:S(2)}) copy-start(f32[8,256,256]{2,1,0:T(8,128)} %blocks_ref.1) | copy-start | bytes 6291460

commit v3 on v2

--- a/solution.py
+++ b/solution.py
@@ -105,9 +105,7 @@
     for d in range(SPAN):
         shift = (REACH - d) % DEVICES
         moved = pltpu.roll(buckets, shift, 1) if shift else buckets
-        for c in range(7):
-            at = c * SPAN * CAP + d * CAP
-            rows_ref[at : at + CAP, :] = moved[c * CAP : (c + 1) * CAP, :]
+        rows_ref[d * 7 * CAP : (d + 1) * 7 * CAP, :] = moved
     for i in range(CHUNKS):
         message_ref[pl.ds(i, DEVICES, stride=CHUNKS), :] = rows_ref[i * 128 : (i + 1) * 128, :].T
 
@@ -130,7 +128,7 @@
         rows_ref[2:3, :] = leaf & 3
         rows_ref[3:4, :] = (leaf + REACH * LEAVES) >> 2
 
-    split_ref[0], split_ref[1] = two(maps_ref[...])
+    split_ref[:, :, : 3 * NEQ], split_ref[:, :, 3 * NEQ :] = two(maps_ref[...])
     leaf_row = iota((128, LANES), 0)
     for k, ref in enumerate((near_hot_ref, own_hot_ref)):
         row = jnp.where(rows_ref[2 * k : 2 * k + 1, :] == step, rows_ref[2 * k + 1 : 2 * k + 2, :], -1)
@@ -156,9 +154,10 @@
             ]
     high, low = two(picked_ref[...])
     weights = jnp.concatenate([high] * GROUPS + [low] * GROUPS, axis=0)
+    weights = jnp.concatenate([weights, weights], axis=1)
     total = jnp.zeros((3 * NEQ, 128), F32)
     for o in range(8):
-        image = dot(maps_ref[0, o], weights, NT) + dot(maps_ref[1, o], weights, NT)
+        image = dot(maps_ref[o], weights, NT)
         total = jnp.where(octants == o, image, total)
     group = iota((1, 128), 1) // LEAVES
     nothing = jnp.zeros((NEQ - FAR, NEQ), F32)
@@ -178,35 +177,43 @@
     arrived_ref, near_hot_ref, own_hot_ref, density_ref, shell_ref, out_ref,
     turned_ref, tree_ref, source_ref, target_ref, partial_ref, back_ref,
 ):
-    entries = SPAN * CAP
-    turned = []
-    for i in range(CHUNKS):
-        turned.append(arrived_ref[pl.ds(i, DEVICES, stride=CHUNKS), :].T)
-    turned = jnp.concatenate(turned, axis=0)
-    for c in range(7):
-        turned_ref[pl.ds(c, entries, stride=8), :] = turned[c * entries : (c + 1) * entries, :]
-    turned_ref[pl.ds(7, entries, stride=8), :] = jnp.zeros((entries, DEVICES), F32)
+    turned = [arrived_ref[pl.ds(i, DEVICES, stride=CHUNKS), :].T for i in range(CHUNKS)]
     tree_ref[SPAN * 32 :, :] = jnp.zeros((1024 - SPAN * 32, 128), F32)
-    low_row = iota((128, 128), 0)
-
-    def place(d, carry):
+    low_row = iota((128, 128), 0).astype(F32).astype(BF16)
+    half_row = [(iota((16, 128), 0) // 8 + k).astype(F32).astype(BF16) for k in (0, 2)]
+    one, zero = jnp.ones((16, 128), BF16), jnp.zeros((16, 128), BF16)
+
+    def narrow(row):
+        return jnp.broadcast_to(row.astype(F32), (16, 128)).astype(BF16)
+
+    def place(d):
         lows, values = [], []
         for r in range(CAP):
-            entry = turned_ref[pl.ds(pl.multiple_of((d * CAP + r) * 8, 8), 8), :]
+            entry = turned_ref[(d * CAP + r) * 8 : (d * CAP + r) * 8 + 8, :]
             slot = entry[6:7, :].astype(jnp.int32) - 1
-            lows.append((low_row == (slot & 127)).astype(F32).astype(BF16))
-            high = slot >> 7
-            parts = three(entry)
+            low, high = narrow(slot & 127), narrow(slot >> 7)
+            lows.append(
+                jnp.concatenate(
+                    [jnp.where(low_row[k : k + 16] == low, one, zero) for k in range(0, 128, 16)],
+                    axis=0,
+                )
+            )
+            here = [row == high for row in half_row]
+            parts = [jnp.concatenate([part, part], axis=0).astype(BF16) for part in three(entry)]
             values.append(
-                jnp.concatenate(
-                    [jnp.where(high == h, part, 0.0) for part in parts for h in range(4)], axis=0
-                ).astype(BF16)
+                jnp.concatenate([jnp.where(h, part, zero) for part in parts for h in here], axis=0)
             )
-        placed = dot(jnp.concatenate(values, axis=1), jnp.concatenate(lows, axis=1), NT)
-        tree_ref[pl.ds(pl.multiple_of(d * 32, 32), 32), :] = thirds(placed, 32)
-        return carry
-
-    lax.fori_loop(0, SPAN, place, 0, unroll=True)
+        placed = dot(jnp.concatenate(lows, axis=1), jnp.concatenate(values, axis=1), NT).T
+        tree_ref[d * 32 : (d + 1) * 32, :] = thirds(placed, 32)
+
+    for d in range(SPAN):
+        for c in range(7):
+            at = d * 7 * CAP + c * CAP
+            turned_ref[pl.ds(d * 8 * CAP + c, CAP, stride=8), :] = turned[at // 128][
+                at % 128 : at % 128 + CAP, :
+            ]
+        turned_ref[pl.ds(d * 8 * CAP + 7, CAP, stride=8), :] = jnp.zeros((CAP, DEVICES), F32)
+        place(d)
 
     terms = [[], [], []]
     for c in range(6):
@@ -263,7 +270,7 @@
                 )
             return carry
 
-        lax.fori_loop(0, LPTS, step, 0, unroll=8)
+        lax.fori_loop(0, LPTS, step, 0, unroll=16)
 
     same = (iota((LEAVES, LANES), 0) == lane_place()[0]).astype(F32).astype(BF16)
     same = jnp.concatenate([same] * 3, axis=1)
@@ -370,7 +377,7 @@
         prepare_kernel,
         grid=(4,),
         out_shape=(
-            jax.ShapeDtypeStruct((2, 8, 384, 384), BF16),
+            jax.ShapeDtypeStruct((8, 384, 768), BF16),
             jax.ShapeDtypeStruct((LANES, LANES), BF16),
             jax.ShapeDtypeStruct((LANES, LANES), BF16),
         ),
@@ -379,7 +386,7 @@
             pl.BlockSpec((2, 384, 384), lambda i: (i, 0, 0)),
         ],
         out_specs=(
-            pl.BlockSpec((2, 2, 384, 384), lambda i: (0, i, 0, 0)),
+            pl.BlockSpec((2, 384, 768), lambda i: (i, 0, 0)),
             pl.BlockSpec((128, LANES), lambda i: (i, 0)),
             pl.BlockSpec((128, LANES), lambda i: (i, 0)),
         ),

time: 58.3 us -> 57.6 us (0.988)
  Pallas kernels: 16.8 us -> 15.8 us
    pallas_call x1, Pallas kernels: 8.1 us -> 7.46 us  [local(): pl.pallas_call(field_kernel, out_shape=shape(DEVICES, 128), scratch_shape...]
where the time goes in v3:
time: 57.6 us; the launch traced here: 57.2 us
  starting transfers between devices  26.9 us (47%)
  Pallas kernels  15.8 us (27%)
  waiting for transfers between devices  9.66 us (17%)
  local copies, waits for them, and re-layouts  4.65 us (8%)
    all_to_all x2, starting transfers between devices, exchange(): lax.all_to_all(rows.reshape(-1), AXES, 0, 0, tiled=True).reshape(rows.shape)  17.2 us
    all_to_all x2, waiting for transfers between devices, exchange(): lax.all_to_all(rows.reshape(-1), AXES, 0, 0, tiled=True).reshape(rows.shape)  9.66 us
    ppermute x2, starting transfers between devices, shifted(): return lax.ppermute(value, AXES, pairs)  9.65 us
    pallas_call x1, Pallas kernels, local(): pl.pallas_call(field_kernel, out_shape=shape(DEVICES, 128), scratch_shape...  7.46 us
    unnamed x22, local copies, waits for them, and re-layouts  4.65 us
    pallas_call x1, Pallas kernels, local(): pl.pallas_call(pack_kernel, out_shape=(shape(CHUNKS * 128, 128), shape(1,...  2.75 us
    pallas_call x1, Pallas kernels, local(): pl.pallas_call(density_kernel, out_shape=shape(3 * LPTS, 128), in_specs=[...  2.04 us
    pallas_call x1, Pallas kernels, local(): pl.pallas_call(fiber_kernel, out_shape=shape(8, 256), scratch_shapes=[plt...  1.3 us
  transfers between devices with their start and end apart: 4, of which 2 were waited for; matrix products, arithmetic and copies ran while one was open for 0% of the time, Pallas kernels for 8%

profile of v3, /device:TPU:1, one launch (start us, length us, event | category | flops | bytes accessed | tf_op | source)
XLA Modules:
  0.0 57.2 jit_solution(9563741977141940437)
XLA Ops:
  0.0 0.0 copy-start.4
  0.0 0.0 copy-start.8
  0.0 0.0 copy-start.2
  0.0 2.8 %pack.1 = (f32[1920,128]{1,0:T(8,128)}, f32[1,512]{1,0:T(1,128)}) custom-call(f32[3,512]{1,0:T(4,128)} %pos_ref.1, f32[3,512]{1,0:T(4,128)} %force_ref.1, s32[1,512]{1,0:T(1,128)} %bitcast.16), custom_call_target="tpu_custom_call" | custom-call | flops 100000000 | bytes 1000000 | tf_op jit(solution)/shard_map/pack/pallas_call | solution.py:362
  2.8 11.5 %all-to-all-start = ((f32[128,1920,1]{1,2,0:T(1,128)}), f32[128,1920,1]{1,2,0:T(1,128)S(1)}, u32[]{:S(2)}, u32[]{:S(2)}) async-start(f32[128,1920,1]{1,2,0:T(1,128)} %bitcast.19), calls=%async_computation | async-start | bytes 1966080 | tf_op jit(solution)/shard_map/all_to_all | solution.py:352
  14.3 3.3 %collective-permute-start = (f32[3,2,128]{2,1,0:T(2,128)}, f32[3,2,128]{2,1,0:T(2,128)S(1)}, u32[]{:S(2)}, u32[]{:S(2)}) collective-permute-start(f32[3,2,128]{2,1,0:T(2,128)} %bitcast.13), channel_id=1, source_target_pairs={{0,1},{1,2},{2,3},{3,4},{4,5},{5,6},{6,7},{7,8},{8,9},{9,10},{10,1... | collective-permute-start | bytes 9224 | tf_op jit(solution)/shard_map/ppermute | solution.py:344
  17.5 6.4 %collective-permute-start.1 = (f32[3,2,128]{2,1,0:T(2,128)}, f32[3,2,128]{2,1,0:T(2,128)S(1)}, u32[]{:S(2)}, u32[]{:S(2)}) collective-permute-start(f32[3,2,128]{2,1,0:T(2,128)} %bitcast.14), channel_id=1, source_target_pairs={{1,0},{2,1},{3,2},{4,3},{5,4},{6,5},{7,6},{8,7},{9,8},{10,9},{11,1... | collective-permute-start | bytes 9224 | tf_op jit(solution)/shard_map/ppermute | solution.py:344
  23.9 0.0 copy-start
  23.9 2.3 %copy-done = f32[8,384,384]{2,1,0:T(8,128)S(1)} copy-done((f32[8,384,384]{2,1,0:T(8,128)S(1)}, f32[8,384,384]{2,1,0:T(8,128)}, u32[]{:S(2)}) %copy-start) | copy-done | bytes 4718616
  26.3 0.7 %copy-done.3 = s32[16,27]{1,0:T(8,128)S(1)} copy-done((s32[16,27]{1,0:T(8,128)S(1)}, s32[16,27]{1,0:T(8,128)}, u32[]{:S(2)}) %copy-start.3) | copy-done | bytes 1752
  27.0 1.3 %prepare.1 = (bf16[8,384,768]{2,1,0:T(8,128)(2,1)S(1)}, bf16[512,512]{1,0:T(8,128)(2,1)S(1)}, bf16[512,512]{1,0:T(8,128)(2,1)S(1)}) custom-call(s32[16,27]{1,0:T(8,128)S(1)} %copy-done.3, f32[8,384,384]{2,1,0:T(8,128)S(1)} %copy-done), custom_call_target="tpu_custom_call" | custom-call | flops 5000000 | bytes 10000000 | tf_op jit(solution)/shard_map/prepare/pallas_call | solution.py:376
  28.3 0.0 collective-permute-done.before_ref
  28.3 0.0 collective-permute-done.1.after_ref
  28.3 0.0 copy-done.4
  28.3 0.0 copy-done.8
  28.3 0.0 copy-done.9
  28.3 0.0 copy-done.2
  28.3 2.0 %density.1.density_ref = f32[96,128]{1,0:T(8,128)S(1)} custom-call(s32[16]{0:T(128)S(1)} %copy-done.8, s32[16]{0:T(128)S(1)} %copy-done.9, f32[3,2,128]{2,1,0:T(2,128)S(1)} %collective-permute-done.before_ref, f32[3,2,128]{2,1,0:T(2,128)S(1)} %bitcast.15, f32[3,2,128]{2,1,0:T(2,128)S(1)} %collective-permute-done.1.after_ref, f32[3,16,128]{2,1,0:T(8,128)S(1)} %bitcast.12, ...), custom_call_target="tpu_custom_call" | custom-call | flops 1000000000 | bytes 5000000 | tf_op jit(solution)/shard_map/density/pallas_call | solution.py:408
  30.4 0.0 copy-start.6
  30.4 0.0 copy-start.7
  30.4 2.4 %all-to-all-done = f32[128,1920,1]{1,2,0:T(1,128)S(1)} async-done(((f32[128,1920,1]{1,2,0:T(1,128)}), f32[128,1920,1]{1,2,0:T(1,128)S(1)}, u32[]{:S(2)}, u32[]{:S(2)}) %all-to-all-start) | async-done | bytes 983072 | tf_op jit(solution)/shard_map/all_to_all | solution.py:352
  32.8 0.0 copy-done.10
  32.8 7.5 %field.1 = f32[128,128]{1,0:T(8,128)} custom-call(f32[1920,128]{1,0:T(8,128)S(1)} %bitcast.10, bf16[512,512]{1,0:T(8,128)(2,1)S(1)} %get-tuple-element.14.near_hot_ref, bf16[512,512]{1,0:T(8,128)(2,1)S(1)} %get-tuple-element.15.own_hot_ref, f32[96,128]{1,0:T(8,128)S(1)} %density.1.density_ref, f32[96,128]{1,0:T(8,128)S(1)} %copy-done.10), custom_call_target="tpu_custom_call" | custom-call | flops 1000000000 | bytes 2000000 | tf_op jit(solution)/shard_map/field/pallas_call | solution.py:423
  40.3 5.8 %all-to-all-start.1 = ((f32[128,128,1]{1,2,0:T(1,128)}), f32[128,128,1]{1,2,0:T(1,128)S(1)}, u32[]{:S(2)}, u32[]{:S(2)}) async-start(f32[128,128,1]{1,2,0:T(1,128)} %bitcast.6), calls=%async_computation.1 | async-start | bytes 131072 | tf_op jit(solution)/shard_map/all_to_all | solution.py:352
  46.1 0.0 copy-start.1
  46.1 1.6 %copy-done.1 = f32[8,256,256]{2,1,0:T(8,128)S(1)} copy-done((f32[8,256,256]{2,1,0:T(8,128)S(1)}, f32[8,256,256]{2,1,0:T(8,128)}, u32[]{:S(2)}) %copy-start.1) | copy-done | bytes 2097176
  47.7 1.0 %split.1.blocks_ref = bf16[2,8,256,256]{3,2,1,0:T(8,128)(2,1)S(1)} custom-call(f32[8,256,256]{2,1,0:T(8,128)S(1)} %copy-done.1), custom_call_target="tpu_custom_call" | custom-call | flops 2000000 | bytes 4000000 | tf_op jit(solution)/shard_map/split/pallas_call | solution.py:398
  48.7 7.2 %all-to-all-done.1 = f32[128,128,1]{1,2,0:T(1,128)S(1)} async-done(((f32[128,128,1]{1,2,0:T(1,128)}), f32[128,128,1]{1,2,0:T(1,128)S(1)}, u32[]{:S(2)}, u32[]{:S(2)}) %all-to-all-start.1) | async-done | bytes 65568 | tf_op jit(solution)/shard_map/all_to_all | solution.py:352
  55.9 0.0 copy-done.5
  55.9 0.0 copy-done.6
  55.9 0.0 copy-done.7
  55.9 1.3 %fiber.1 = f32[8,256]{1,0:T(8,128)} custom-call(f32[128,128]{1,0:T(8,128)S(1)} %bitcast.11, s32[1,512]{1,0:T(1,128)S(1)} %bitcast.17, f32[1,512]{1,0:T(1,128)S(1)} %copy-done.7, f32[1,512]{1,0:T(1,128)S(1)} %bitcast.18, bf16[2,8,256,256]{3,2,1,0:T(8,128)(2,1)S(1)} %split.1.blocks_ref), custom_call_target="tpu_custom_call" | custom-call | flops 100000000 | bytes 2000000 | tf_op jit(solution)/shard_map/fiber/pallas_call | solution.py:439
  (4 shorter events, 0.0 us)
Async XLA Ops:
  0.0 28.3 %copy-start.4 = (f32[2,3,128]{2,0,1:T(2,128)S(1)}, f32[2,3,128]{2,0,1:T(2,128)}, u32[]{:S(2)}) copy-start(f32[2,3,128]{2,0,1:T(2,128)} %param.17) | copy-start | bytes 9220
  0.0 28.3 %copy-start.8 = (s32[16]{0:T(128)S(1)}, s32[16]{0:T(128)}, u32[]{:S(2)}) copy-start(s32[16]{0:T(128)} %parent_ref.1) | copy-start | bytes 196
  0.0 28.3 %copy-start.9 = (s32[16]{0:T(128)S(1)}, s32[16]{0:T(128)}, u32[]{:S(2)}) copy-start(s32[16]{0:T(128)} %octant_ref.1) | copy-start | bytes 196
  0.0 28.3 %copy-start.2 = (f32[16,3,128]{2,0,1:T(8,128)S(1)}, f32[16,3,128]{2,0,1:T(8,128)}, u32[]{:S(2)}) copy-start(f32[16,3,128]{2,0,1:T(8,128)} %param.16) | copy-start | bytes 73732
  2.8 30.1 %copy-start.10 = (f32[96,128]{1,0:T(8,128)S(1)}, f32[96,128]{1,0:T(8,128)}, u32[]{:S(2)}) copy-start(f32[96,128]{1,0:T(8,128)} %constant.2.clone.shell_ref) | copy-start | bytes 147460
  2.8 30.1 %all-to-all-start = ((f32[128,1920,1]{1,2,0:T(1,128)}), f32[128,1920,1]{1,2,0:T(1,128)S(1)}, u32[]{:S(2)}, u32[]{:S(2)}) async-start(f32[128,1920,1]{1,2,0:T(1,128)} %bitcast.19), calls=%async_computation | async-start | bytes 1966080 | tf_op jit(solution)/shard_map/all_to_all | solution.py:352
  14.3 14.0 %collective-permute-start = (f32[3,2,128]{2,1,0:T(2,128)}, f32[3,2,128]{2,1,0:T(2,128)S(1)}, u32[]{:S(2)}, u32[]{:S(2)}) collective-permute-start(f32[3,2,128]{2,1,0:T(2,128)} %bitcast.13), channel_id=1, source_target_pairs={{0,1},{1,2},{2,3},{3,4},{4,5},{5,6},{6,7},{7,8},{8,9},{9,10},{10,1... | collective-permute-start | bytes 9224 | tf_op jit(solution)/shard_map/ppermute | solution.py:344
  17.5 10.7 %collective-permute-start.1 = (f32[3,2,128]{2,1,0:T(2,128)}, f32[3,2,128]{2,1,0:T(2,128)S(1)}, u32[]{:S(2)}, u32[]{:S(2)}) collective-permute-start(f32[3,2,128]{2,1,0:T(2,128)} %bitcast.14), channel_id=1, source_target_pairs={{1,0},{2,1},{3,2},{4,3},{5,4},{6,5},{7,6},{8,7},{9,8},{10,9},{11,1... | collective-permute-start | bytes 9224 | tf_op jit(solution)/shard_map/ppermute | solution.py:344
  23.9 2.3 %copy-start = (f32[8,384,384]{2,1,0:T(8,128)S(1)}, f32[8,384,384]{2,1,0:T(8,128)}, u32[]{:S(2)}) copy-start(f32[8,384,384]{2,1,0:T(8,128)} %maps_ref.1) | copy-start | bytes 14155780
  26.3 0.7 %copy-start.3 = (s32[16,27]{1,0:T(8,128)S(1)}, s32[16,27]{1,0:T(8,128)}, u32[]{:S(2)}) copy-start(s32[16,27]{1,0:T(8,128)} %near_ref.1) | copy-start | bytes 5188
  30.4 25.5 %copy-start.5 = (s32[512]{0:T(512)S(1)}, s32[512]{0:T(512)}, u32[]{:S(2)}) copy-start(s32[512]{0:T(512)} %param.15) | copy-start | bytes 6148
  30.4 25.5 %copy-start.6 = (f32[512]{0:T(512)S(1)}, f32[512]{0:T(512)}, u32[]{:S(2)}) copy-start(f32[512]{0:T(512)} %param.14) | copy-start | bytes 6148
  30.4 25.5 %copy-start.7 = (f32[1,512]{1,0:T(1,128)S(1)}, f32[1,512]{1,0:T(1,128)}, u32[]{:S(2)}) copy-start(f32[1,512]{1,0:T(1,128)} %get-tuple-element.18.rank_ref) | copy-start | bytes 6148
  40.3 15.6 %all-to-all-start.1 = ((f32[128,128,1]{1,2,0:T(1,128)}), f32[128,128,1]{1,2,0:T(1,128)S(1)}, u32[]{:S(2)}, u32[]{:S(2)}) async-start(f32[128,128,1]{1,2,0:T(1,128)} %bitcast.6), calls=%async_computation.1 | async-start | bytes 131072 | tf_op jit(solution)/shard_map/all_to_all | solution.py:352
  46.1 1.6 %copy-start.1 = (f32[8,256,256]{2,1,0:T(8,128)S(1)}, f32[8,256,256]{2,1,0:T(8,128)}, u32[]{:S(2)}) copy-start(f32[8,256,256]{2,1,0:T(8,128)} %blocks_ref.1) | copy-start | bytes 6291460

commit v4 on v3

--- a/solution.py
+++ b/solution.py
@@ -91,8 +91,16 @@
     slot = slot_ref[...]
     hot = owner_hot(slot)
     hot_b = hot.astype(BF16)
-    before = (iota((NODES, NODES), 0) < iota((NODES, NODES), 1)).astype(F32).astype(BF16)
-    rank = jnp.sum(hot * dot(hot_b, before, NN), axis=0, keepdims=True)
+    row, column = iota((128, 256), 0), iota((128, 256), 1)
+    before = ((row < column) | (column >= 128)).astype(F32).astype(BF16)
+    earlier = jnp.zeros((DEVICES, 128), F32)
+    ranks = []
+    for k in range(NODES // 128):
+        lanes = slice(k * 128, (k + 1) * 128)
+        counts = dot(hot_b[:, lanes], before, NN)
+        ranks.append(jnp.sum(hot[:, lanes] * (counts[:, :128] + earlier), axis=0, keepdims=True))
+        earlier = earlier + counts[:, 128:]
+    rank = jnp.concatenate(ranks, axis=1)
     rank_ref[...] = rank
     here = iota((CAP, NODES), 0).astype(F32) == rank
     within = (slot & (NODES - 1)).astype(F32) + 1.0
@@ -110,67 +118,63 @@
         message_ref[pl.ds(i, DEVICES, stride=CHUNKS), :] = rows_ref[i * 128 : (i + 1) * 128, :].T
 
 
-def prepare_kernel(near_ref, maps_ref, split_ref, near_hot_ref, own_hot_ref, rows_ref):
-    step = pl.program_id(0)
-
-    @pl.when(step == 0)
-    def _():
-        leaf, place = lane_place()
-        near = near_ref[...] - LEAVES * (device_index() - REACH)
-        spread = (iota((NEAR, LANES), 0) == place).astype(F32).astype(BF16)
-        own = iota((LEAVES, LANES), 0) == leaf
-        values = jnp.concatenate([near & 3, near >> 2], axis=0).astype(F32).astype(BF16)
-        values = dot(values, spread, NN)
-        for k in range(2):
-            value = jnp.where(own, values[k * LEAVES : (k + 1) * LEAVES], 0.0)
-            value = jnp.sum(value, axis=0, keepdims=True).astype(jnp.int32)
-            rows_ref[k : k + 1, :] = jnp.where(place >= 0, value, -1)
-        rows_ref[2:3, :] = leaf & 3
-        rows_ref[3:4, :] = (leaf + REACH * LEAVES) >> 2
-
-    split_ref[:, :, : 3 * NEQ], split_ref[:, :, 3 * NEQ :] = two(maps_ref[...])
+def prepare_kernel(near_ref, local_ref, maps_ref, near_hot_ref, own_hot_ref, placed_ref, held_ref):
+    held_ref[...] = maps_ref[...]
+    leaf, place = lane_place()
+    near = near_ref[...] - LEAVES * (device_index() - REACH)
+    spread = (iota((NEAR, LANES), 0) == place).astype(F32).astype(BF16)
+    own = iota((LEAVES, LANES), 0) == leaf
+    values = jnp.concatenate([near & 3, near >> 2], axis=0).astype(F32).astype(BF16)
+    values = dot(values, spread, NN)
+    rows = []
+    for k in range(2):
+        value = jnp.where(own, values[k * LEAVES : (k + 1) * LEAVES], 0.0)
+        value = jnp.sum(value, axis=0, keepdims=True).astype(jnp.int32)
+        rows.append(jnp.where(place >= 0, value, -1))
     leaf_row = iota((128, LANES), 0)
-    for k, ref in enumerate((near_hot_ref, own_hot_ref)):
-        row = jnp.where(rows_ref[2 * k : 2 * k + 1, :] == step, rows_ref[2 * k + 1 : 2 * k + 2, :], -1)
-        ref[...] = (leaf_row == row).astype(F32).astype(BF16)
+    picks = ((near_hot_ref, *rows), (own_hot_ref, leaf & 3, (leaf + REACH * LEAVES) >> 2))
+    for ref, quarter, row in picks:
+        for w in range(4):
+            here = leaf_row == jnp.where(quarter == w, row, -1)
+            ref[w * 128 : (w + 1) * 128, :] = here.astype(F32).astype(BF16)
+    group = iota((1, 128), 1) // LEAVES
+    nothing = jnp.zeros((NEQ - FAR, NEQ), F32)
+    for c in range(3):
+        local = jnp.concatenate([local_ref[c]] * GROUPS + [nothing], axis=0).T
+        placed = jnp.zeros((LPTS, 128), F32)
+        for g in range(GROUPS):
+            placed = jnp.where(group == g, local[g * LPTS : (g + 1) * LPTS], placed)
+        placed_ref[c * LPTS : (c + 1) * LPTS, :] = placed
 
 
 def density_kernel(
-    parent_ref, octant_ref, before_ref, own_ref, after_ref, local_ref, maps_ref, out_ref,
-    six_ref, picked_ref,
+    parent_ref, octant_ref, before_ref, own_ref, after_ref, placed_ref, maps_ref, out_ref, six_ref
 ):
     first_parent = 2 * (device_index() - 1)
     for j in range(6):
         source = (before_ref, own_ref, after_ref)[j // 2]
         for c in range(3):
             six_ref[c * 8 + j : c * 8 + j + 1, :] = source[c, j % 2 : j % 2 + 1, :]
-    lane = iota((1, 128), 1) % LEAVES
-    octants = jnp.zeros((1, 128), jnp.int32)
-    for l in range(LEAVES):
-        octants = jnp.where(lane == l, octant_ref[l], octants)
+    out_ref[...] = jnp.zeros_like(out_ref)
+    lane = iota((1, 128), 1)
+
+    def translate(l, carry):
+        octant, at = octant_ref[l], parent_ref[l] - first_parent
+        parent = [six_ref[pl.ds(c * 8 + at, 1), :] for c in range(3)]
         for c in range(3):
-            picked_ref[l : l + 1, c * NEQ : (c + 1) * NEQ] = six_ref[
-                pl.ds(c * 8 + parent_ref[l] - first_parent, 1), :
-            ]
-    high, low = two(picked_ref[...])
-    weights = jnp.concatenate([high] * GROUPS + [low] * GROUPS, axis=0)
-    weights = jnp.concatenate([weights, weights], axis=1)
-    total = jnp.zeros((3 * NEQ, 128), F32)
-    for o in range(8):
-        image = dot(maps_ref[o], weights, NT)
-        total = jnp.where(octants == o, image, total)
-    group = iota((1, 128), 1) // LEAVES
-    nothing = jnp.zeros((NEQ - FAR, NEQ), F32)
-    for c in range(3):
-        local = jnp.concatenate([local_ref[c]] * GROUPS + [nothing], axis=0).T
-        moved = total[c * NEQ : (c + 1) * NEQ]
-        placed = jnp.zeros((LPTS, 128), F32)
-        for g in range(GROUPS):
-            rows = slice(g * LPTS, (g + 1) * LPTS)
-            here = group % GROUPS == g
-            placed = jnp.where(here, moved[rows] + local[rows], placed)
-        placed = placed + pltpu.roll(placed, 128 - FAR, 1)
-        out_ref[c * LPTS : (c + 1) * LPTS, :] = jnp.where(group < GROUPS, placed, 0.0)
+            out = out_ref[c * LPTS : (c + 1) * LPTS, :]
+            for g in range(GROUPS):
+                rows = slice(c * NEQ + g * LPTS, c * NEQ + (g + 1) * LPTS)
+                image = maps_ref[octant, rows, :NEQ] * parent[0]
+                image = image + maps_ref[octant, rows, NEQ : 2 * NEQ] * parent[1]
+                image = image + maps_ref[octant, rows, 2 * NEQ :] * parent[2]
+                image = jnp.sum(image, axis=1, keepdims=True)
+                out = jnp.where(lane == g * LEAVES + l, image, out)
+            out_ref[c * LPTS : (c + 1) * LPTS, :] = out
+        return carry
+
+    lax.fori_loop(0, LEAVES, translate, 0, unroll=8)
+    out_ref[...] += placed_ref[...]
 
 
 def field_kernel(
@@ -373,28 +377,18 @@
 
     vmem = pl.BlockSpec(memory_space=pltpu.VMEM)
     smem = pl.BlockSpec(memory_space=pltpu.SMEM)
-    maps, near_hot, own_hot = pl.pallas_call(
+    near_hot, own_hot, placed, maps = pl.pallas_call(
         prepare_kernel,
-        grid=(4,),
         out_shape=(
-            jax.ShapeDtypeStruct((8, 384, 768), BF16),
             jax.ShapeDtypeStruct((LANES, LANES), BF16),
             jax.ShapeDtypeStruct((LANES, LANES), BF16),
+            shape(3 * LPTS, 128),
+            shape(8, 3 * NEQ, 3 * NEQ),
         ),
-        in_specs=[
-            pl.BlockSpec((LEAVES, NEAR), lambda i: (0, 0)),
-            pl.BlockSpec((2, 384, 384), lambda i: (i, 0, 0)),
-        ],
-        out_specs=(
-            pl.BlockSpec((2, 384, 768), lambda i: (i, 0, 0)),
-            pl.BlockSpec((128, LANES), lambda i: (i, 0)),
-            pl.BlockSpec((128, LANES), lambda i: (i, 0)),
-        ),
-        scratch_shapes=[pltpu.VMEM((8, LANES), jnp.int32)],
         cost_estimate=pl.CostEstimate(flops=5 * 10**6, bytes_accessed=10**7, transcendentals=0),
         compiler_params=grant(8),
         name="prepare",
-    )(near_list, l2l_maps)
+    )(near_list, leaf_local, l2l_maps)
     split = pl.pallas_call(
         split_kernel,
         grid=(4,),
@@ -409,16 +403,13 @@
         density_kernel,
         out_shape=shape(3 * LPTS, 128),
         in_specs=[smem, smem, vmem, vmem, vmem, vmem, vmem],
-        scratch_shapes=[
-            pltpu.VMEM((24, NEQ), F32),
-            pltpu.VMEM((LEAVES, 3 * NEQ), F32),
-        ],
+        scratch_shapes=[pltpu.VMEM((24, NEQ), F32)],
         cost_estimate=pl.CostEstimate(flops=10**9, bytes_accessed=5 * 10**6, transcendentals=0),
         compiler_params=grant(16),
         name="density",
     )(
         leaf_parent, leaf_octant, from_before, parent_local, from_after,
-        leaf_local, maps,
+        placed, maps,
     )
     back = pl.pallas_call(
         field_kernel,

time: 57.6 us -> 57.1 us (level)
  Pallas kernels: 15.8 us -> 14.7 us
  local copies, waits for them, and re-layouts: 4.65 us -> 5.39 us
    unnamed x22, local copies, waits for them, and re-layouts: 4.65 us -> 5.39 us
    pallas_call x1, Pallas kernels: 1.29 us -> 0.64 us  [local(): pl.pallas_call(prepare_kernel, out_shape=(jax.ShapeDtypeStruct((LANES, LA...]
  transfers between devices with their start and end apart: 4 -> 4, of which waited for: 2 -> 2; matrix products, arithmetic and copies ran while one was open for 0% -> 0% of each run, Pallas kernels for 8% -> 6%
where the time goes in v4:
time: 57.1 us; the launch traced here: 56.6 us
  starting transfers between devices  26.4 us (46%)
  Pallas kernels  14.7 us (26%)
  waiting for transfers between devices  10.1 us (18%)
  local copies, waits for them, and re-layouts  5.39 us (9%)
    all_to_all x2, starting transfers between devices, exchange(): lax.all_to_all(rows.reshape(-1), AXES, 0, 0, tiled=True).reshape(rows.shape)  16.8 us
    all_to_all x2, waiting for transfers between devices, exchange(): lax.all_to_all(rows.reshape(-1), AXES, 0, 0, tiled=True).reshape(rows.shape)  10.1 us
    ppermute x2, starting transfers between devices, shifted(): return lax.ppermute(value, AXES, pairs)  9.65 us
    pallas_call x1, Pallas kernels, local(): pl.pallas_call(field_kernel, out_shape=shape(DEVICES, 128), scratch_shape...  7.46 us
    unnamed x22, local copies, waits for them, and re-layouts  5.39 us
    pallas_call x1, Pallas kernels, local(): pl.pallas_call(pack_kernel, out_shape=(shape(CHUNKS * 128, 128), shape(1,...  2.71 us
    pallas_call x1, Pallas kernels, local(): pl.pallas_call(density_kernel, out_shape=shape(3 * LPTS, 128), in_specs=[...  1.55 us
    pallas_call x1, Pallas kernels, local(): pl.pallas_call(fiber_kernel, out_shape=shape(8, 256), scratch_shapes=[plt...  1.3 us
  transfers between devices with their start and end apart: 4, of which 2 were waited for; matrix products, arithmetic and copies ran while one was open for 0% of the time, Pallas kernels for 6%

profile of v4, /device:TPU:1, one launch (start us, length us, event | category | flops | bytes accessed | tf_op | source)
XLA Modules:
  0.0 56.6 jit_solution(9153836824671318642)
XLA Ops:
  0.0 0.0 copy-start.4
  0.0 0.0 copy-start.8
  0.0 2.7 %pack.1 = (f32[1920,128]{1,0:T(8,128)}, f32[1,512]{1,0:T(1,128)}) custom-call(f32[3,512]{1,0:T(4,128)} %pos_ref.1, f32[3,512]{1,0:T(4,128)} %force_ref.1, s32[1,512]{1,0:T(1,128)} %bitcast.16), custom_call_target="tpu_custom_call" | custom-call | flops 100000000 | bytes 1000000 | tf_op jit(solution)/shard_map/pack/pallas_call | solution.py:366
  2.7 11.5 %all-to-all-start = ((f32[128,1920,1]{1,2,0:T(1,128)}), f32[128,1920,1]{1,2,0:T(1,128)S(1)}, u32[]{:S(2)}, u32[]{:S(2)}) async-start(f32[128,1920,1]{1,2,0:T(1,128)} %bitcast.19), calls=%async_computation | async-start | bytes 1966080 | tf_op jit(solution)/shard_map/all_to_all | solution.py:356
  14.2 3.3 %collective-permute-start = (f32[3,2,128]{2,1,0:T(2,128)}, f32[3,2,128]{2,1,0:T(2,128)S(1)}, u32[]{:S(2)}, u32[]{:S(2)}) collective-permute-start(f32[3,2,128]{2,1,0:T(2,128)} %bitcast.13), channel_id=1, source_target_pairs={{0,1},{1,2},{2,3},{3,4},{4,5},{5,6},{6,7},{7,8},{8,9},{9,10},{10,1... | collective-permute-start | bytes 9224 | tf_op jit(solution)/shard_map/ppermute | solution.py:348
  17.5 6.4 %collective-permute-start.1 = (f32[3,2,128]{2,1,0:T(2,128)}, f32[3,2,128]{2,1,0:T(2,128)S(1)}, u32[]{:S(2)}, u32[]{:S(2)}) collective-permute-start(f32[3,2,128]{2,1,0:T(2,128)} %bitcast.14), channel_id=1, source_target_pairs={{1,0},{2,1},{3,2},{4,3},{5,4},{6,5},{7,6},{8,7},{9,8},{10,9},{11,1... | collective-permute-start | bytes 9224 | tf_op jit(solution)/shard_map/ppermute | solution.py:348
  23.9 0.0 copy-start
  23.9 2.3 %copy-done = f32[8,384,384]{2,1,0:T(8,128)S(1)} copy-done((f32[8,384,384]{2,1,0:T(8,128)S(1)}, f32[8,384,384]{2,1,0:T(8,128)}, u32[]{:S(2)}) %copy-start) | copy-done | bytes 4718616
  26.2 0.7 %copy-done.2 = f32[16,3,128]{2,0,1:T(8,128)S(1)} copy-done((f32[16,3,128]{2,0,1:T(8,128)S(1)}, f32[16,3,128]{2,0,1:T(8,128)}, u32[]{:S(2)}) %copy-start.2) | copy-done | bytes 24600
  27.0 0.7 %copy-done.3 = s32[16,27]{1,0:T(8,128)S(1)} copy-done((s32[16,27]{1,0:T(8,128)S(1)}, s32[16,27]{1,0:T(8,128)}, u32[]{:S(2)}) %copy-start.3) | copy-done | bytes 1752
  27.7 0.6 %prepare.1 = (bf16[512,512]{1,0:T(8,128)(2,1)S(1)}, bf16[512,512]{1,0:T(8,128)(2,1)S(1)}, f32[96,128]{1,0:T(8,128)S(1)}, f32[8,384,384]{2,1,0:T(8,128)S(1)}) custom-call(s32[16,27]{1,0:T(8,128)S(1)} %copy-done.3, f32[3,16,128]{2,1,0:T(8,128)S(1)} %bitcast.12, f32[8,384,384]{2,1,0:T(8,128)S(1)} %copy-done), custom_call_target="tpu_custom_call" | custom-call | flops 5000000 | bytes 10000000 | tf_op jit(solution)/shard_map/prepare/pallas_call | solution.py:380
  28.3 0.0 collective-permute-done.before_ref
  28.3 0.0 collective-permute-done.1.after_ref
  28.3 0.0 copy-done.4
  28.3 0.0 copy-done.8
  28.3 0.0 copy-done.9
  28.4 1.6 %density.1.density_ref = f32[96,128]{1,0:T(8,128)S(1)} custom-call(s32[16]{0:T(128)S(1)} %copy-done.8, s32[16]{0:T(128)S(1)} %copy-done.9, f32[3,2,128]{2,1,0:T(2,128)S(1)} %collective-permute-done.before_ref, f32[3,2,128]{2,1,0:T(2,128)S(1)} %bitcast.15, f32[3,2,128]{2,1,0:T(2,128)S(1)} %collective-permute-done.1.after_ref, ...), custom_call_target="tpu_custom_call" | custom-call | flops 1000000000 | bytes 5000000 | tf_op jit(solution)/shard_map/density/pallas_call | solution.py:402
  29.9 0.0 copy-start.5
  29.9 0.0 copy-start.6
  29.9 0.0 copy-start.7
  30.0 2.8 %all-to-all-done = f32[128,1920,1]{1,2,0:T(1,128)S(1)} async-done(((f32[128,1920,1]{1,2,0:T(1,128)}), f32[128,1920,1]{1,2,0:T(1,128)S(1)}, u32[]{:S(2)}, u32[]{:S(2)}) %all-to-all-start) | async-done | bytes 983072 | tf_op jit(solution)/shard_map/all_to_all | solution.py:356
  32.8 0.0 copy-done.10
  32.8 7.5 %field.1 = f32[128,128]{1,0:T(8,128)} custom-call(f32[1920,128]{1,0:T(8,128)S(1)} %bitcast.10, bf16[512,512]{1,0:T(8,128)(2,1)S(1)} %get-tuple-element.15.near_hot_ref, bf16[512,512]{1,0:T(8,128)(2,1)S(1)} %get-tuple-element.16.own_hot_ref, f32[96,128]{1,0:T(8,128)S(1)} %density.1.density_ref, f32[96,128]{1,0:T(8,128)S(1)} %copy-done.10), custom_call_target="tpu_custom_call" | custom-call | flops 1000000000 | bytes 2000000 | tf_op jit(solution)/shard_map/field/pallas_call | solution.py:414
  40.3 5.3 %all-to-all-start.1 = ((f32[128,128,1]{1,2,0:T(1,128)}), f32[128,128,1]{1,2,0:T(1,128)S(1)}, u32[]{:S(2)}, u32[]{:S(2)}) async-start(f32[128,128,1]{1,2,0:T(1,128)} %bitcast.6), calls=%async_computation.1 | async-start | bytes 131072 | tf_op jit(solution)/shard_map/all_to_all | solution.py:356
  45.5 0.0 copy-start.1
  45.5 1.6 %copy-done.1 = f32[8,256,256]{2,1,0:T(8,128)S(1)} copy-done((f32[8,256,256]{2,1,0:T(8,128)S(1)}, f32[8,256,256]{2,1,0:T(8,128)}, u32[]{:S(2)}) %copy-start.1) | copy-done | bytes 2097176
  47.1 1.0 %split.1.blocks_ref = bf16[2,8,256,256]{3,2,1,0:T(8,128)(2,1)S(1)} custom-call(f32[8,256,256]{2,1,0:T(8,128)S(1)} %copy-done.1), custom_call_target="tpu_custom_call" | custom-call | flops 2000000 | bytes 4000000 | tf_op jit(solution)/shard_map/split/pallas_call | solution.py:392
  48.1 7.2 %all-to-all-done.1 = f32[128,128,1]{1,2,0:T(1,128)S(1)} async-done(((f32[128,128,1]{1,2,0:T(1,128)}), f32[128,128,1]{1,2,0:T(1,128)S(1)}, u32[]{:S(2)}, u32[]{:S(2)}) %all-to-all-start.1) | async-done | bytes 65568 | tf_op jit(solution)/shard_map/all_to_all | solution.py:356
  55.3 0.0 copy-done.5
  55.3 0.0 copy-done.6
  55.3 0.0 copy-done.7
  55.3 1.3 %fiber.1 = f32[8,256]{1,0:T(8,128)} custom-call(f32[128,128]{1,0:T(8,128)S(1)} %bitcast.11, s32[1,512]{1,0:T(1,128)S(1)} %bitcast.17, f32[1,512]{1,0:T(1,128)S(1)} %copy-done.7, f32[1,512]{1,0:T(1,128)S(1)} %bitcast.18, bf16[2,8,256,256]{3,2,1,0:T(8,128)(2,1)S(1)} %split.1.blocks_ref), custom_call_target="tpu_custom_call" | custom-call | flops 100000000 | bytes 2000000 | tf_op jit(solution)/shard_map/fiber/pallas_call | solution.py:430
  (4 shorter events, 0.0 us)
Async XLA Ops:
  0.0 28.3 %copy-start.4 = (f32[2,3,128]{2,0,1:T(2,128)S(1)}, f32[2,3,128]{2,0,1:T(2,128)}, u32[]{:S(2)}) copy-start(f32[2,3,128]{2,0,1:T(2,128)} %param.17) | copy-start | bytes 9220
  0.0 28.3 %copy-start.8 = (s32[16]{0:T(128)S(1)}, s32[16]{0:T(128)}, u32[]{:S(2)}) copy-start(s32[16]{0:T(128)} %parent_ref.1) | copy-start | bytes 196
  0.0 28.3 %copy-start.9 = (s32[16]{0:T(128)S(1)}, s32[16]{0:T(128)}, u32[]{:S(2)}) copy-start(s32[16]{0:T(128)} %octant_ref.1) | copy-start | bytes 196
  2.7 30.1 %all-to-all-start = ((f32[128,1920,1]{1,2,0:T(1,128)}), f32[128,1920,1]{1,2,0:T(1,128)S(1)}, u32[]{:S(2)}, u32[]{:S(2)}) async-start(f32[128,1920,1]{1,2,0:T(1,128)} %bitcast.19), calls=%async_computation | async-start | bytes 1966080 | tf_op jit(solution)/shard_map/all_to_all | solution.py:356
  14.2 14.1 %collective-permute-start = (f32[3,2,128]{2,1,0:T(2,128)}, f32[3,2,128]{2,1,0:T(2,128)S(1)}, u32[]{:S(2)}, u32[]{:S(2)}) collective-permute-start(f32[3,2,128]{2,1,0:T(2,128)} %bitcast.13), channel_id=1, source_target_pairs={{0,1},{1,2},{2,3},{3,4},{4,5},{5,6},{6,7},{7,8},{8,9},{9,10},{10,1... | collective-permute-start | bytes 9224 | tf_op jit(solution)/shard_map/ppermute | solution.py:348
  17.5 10.8 %collective-permute-start.1 = (f32[3,2,128]{2,1,0:T(2,128)}, f32[3,2,128]{2,1,0:T(2,128)S(1)}, u32[]{:S(2)}, u32[]{:S(2)}) collective-permute-start(f32[3,2,128]{2,1,0:T(2,128)} %bitcast.14), channel_id=1, source_target_pairs={{1,0},{2,1},{3,2},{4,3},{5,4},{6,5},{7,6},{8,7},{9,8},{10,9},{11,1... | collective-permute-start | bytes 9224 | tf_op jit(solution)/shard_map/ppermute | solution.py:348
  23.9 2.3 %copy-start = (f32[8,384,384]{2,1,0:T(8,128)S(1)}, f32[8,384,384]{2,1,0:T(8,128)}, u32[]{:S(2)}) copy-start(f32[8,384,384]{2,1,0:T(8,128)} %maps_ref.1) | copy-start | bytes 14155780
  26.2 0.7 %copy-start.2 = (f32[16,3,128]{2,0,1:T(8,128)S(1)}, f32[16,3,128]{2,0,1:T(8,128)}, u32[]{:S(2)}) copy-start(f32[16,3,128]{2,0,1:T(8,128)} %param.16) | copy-start | bytes 73732
  27.0 0.7 %copy-start.3 = (s32[16,27]{1,0:T(8,128)S(1)}, s32[16,27]{1,0:T(8,128)}, u32[]{:S(2)}) copy-start(s32[16,27]{1,0:T(8,128)} %near_ref.1) | copy-start | bytes 5188
  27.7 5.1 %copy-start.10 = (f32[96,128]{1,0:T(8,128)S(1)}, f32[96,128]{1,0:T(8,128)}, u32[]{:S(2)}) copy-start(f32[96,128]{1,0:T(8,128)} %constant.2.clone.shell_ref) | copy-start | bytes 147460
  29.9 25.4 %copy-start.5 = (s32[512]{0:T(512)S(1)}, s32[512]{0:T(512)}, u32[]{:S(2)}) copy-start(s32[512]{0:T(512)} %param.15) | copy-start | bytes 6148
  29.9 25.4 %copy-start.6 = (f32[512]{0:T(512)S(1)}, f32[512]{0:T(512)}, u32[]{:S(2)}) copy-start(f32[512]{0:T(512)} %param.14) | copy-start | bytes 6148
  29.9 25.4 %copy-start.7 = (f32[1,512]{1,0:T(1,128)S(1)}, f32[1,512]{1,0:T(1,128)}, u32[]{:S(2)}) copy-start(f32[1,512]{1,0:T(1,128)} %get-tuple-element.20.rank_ref) | copy-start | bytes 6148
  40.3 15.1 %all-to-all-start.1 = ((f32[128,128,1]{1,2,0:T(1,128)}), f32[128,128,1]{1,2,0:T(1,128)S(1)}, u32[]{:S(2)}, u32[]{:S(2)}) async-start(f32[128,128,1]{1,2,0:T(1,128)} %bitcast.6), calls=%async_computation.1 | async-start | bytes 131072 | tf_op jit(solution)/shard_map/all_to_all | solution.py:356
  45.5 1.6 %copy-start.1 = (f32[8,256,256]{2,1,0:T(8,128)S(1)}, f32[8,256,256]{2,1,0:T(8,128)}, u32[]{:S(2)}) copy-start(f32[8,256,256]{2,1,0:T(8,128)} %blocks_ref.1) | copy-start | bytes 6291460

commit v5 on v4

--- a/solution.py
+++ b/solution.py
@@ -173,7 +173,7 @@
             out_ref[c * LPTS : (c + 1) * LPTS, :] = out
         return carry
 
-    lax.fori_loop(0, LEAVES, translate, 0, unroll=8)
+    lax.fori_loop(0, LEAVES, translate, 0, unroll=True)
     out_ref[...] += placed_ref[...]
 
 
@@ -255,26 +255,32 @@
         lanes = slice(chunk * 128, (chunk + 1) * 128)
         soft_c = soft[:, lanes]
 
-        def step(p, carry):
-            aim = [target_ref[pl.ds(chunk * 96 + c * LPTS + p, 1), :] for c in range(3)]
-            sums = None
+        def step(i, carry):
+            first = i * 8
+            sums = [None] * 8
+            aims = [
+                [target_ref[pl.ds(chunk * 96 + c * LPTS + first + k, 1), :] for c in range(3)]
+                for k in range(8)
+            ]
             for g in range(LPTS // 8):
                 at = [source_ref[c * LPTS + g * 8 : c * LPTS + g * 8 + 8, lanes] for c in range(6)]
-                gap = [aim[c] - at[c] for c in range(3)]
-                square = gap[0] * gap[0] + gap[1] * gap[1] + gap[2] * gap[2] + soft_c
-                inverse = lax.rsqrt(square)
-                cube = inverse * inverse * inverse
-                along = (gap[0] * at[3] + gap[1] * at[4] + gap[2] * at[5]) * cube
-                plain = (square + soft_c) * cube
-                new = [plain * at[3 + c] + gap[c] * along for c in range(3)]
-                sums = new if sums is None else [a + b for a, b in zip(sums, new)]
-            for c in range(3):
-                partial_ref[pl.ds(chunk * 96 + c * LPTS + p, 1), :] = jnp.sum(
-                    sums[c], axis=0, keepdims=True
-                )
+                for k in range(8):
+                    gap = [aims[k][c] - at[c] for c in range(3)]
+                    square = gap[0] * gap[0] + gap[1] * gap[1] + gap[2] * gap[2] + soft_c
+                    inverse = lax.rsqrt(square)
+                    cube = inverse * inverse * inverse
+                    along = (gap[0] * at[3] + gap[1] * at[4] + gap[2] * at[5]) * cube
+                    plain = (square + soft_c) * cube
+                    new = [plain * at[3 + c] + gap[c] * along for c in range(3)]
+                    sums[k] = new if sums[k] is None else [a + b for a, b in zip(sums[k], new)]
+            for k in range(8):
+                for c in range(3):
+                    partial_ref[pl.ds(chunk * 96 + c * LPTS + first + k, 1), :] = jnp.sum(
+                        sums[k][c], axis=0, keepdims=True
+                    )
             return carry
 
-        lax.fori_loop(0, LPTS, step, 0, unroll=16)
+        lax.fori_loop(0, LPTS // 8, step, 0, unroll=2)
 
     same = (iota((LEAVES, LANES), 0) == lane_place()[0]).astype(F32).astype(BF16)
     same = jnp.concatenate([same] * 3, axis=1)

time: 57.1 us -> 57 us (level)
  transfers between devices with their start and end apart: 4 -> 4, of which waited for: 2 -> 2; matrix products, arithmetic and copies ran while one was open for 0% -> 0% of each run, Pallas kernels for 6% -> 5%
where the time goes in v5:
time: 57 us; the launch traced here: 56.5 us
  starting transfers between devices  26.3 us (46%)
  Pallas kernels  14.6 us (26%)
  waiting for transfers between devices  10.1 us (18%)
  local copies, waits for them, and re-layouts  5.39 us (9%)
    all_to_all x2, starting transfers between devices, exchange(): lax.all_to_all(rows.reshape(-1), AXES, 0, 0, tiled=True).reshape(rows.shape)  16.7 us
    all_to_all x2, waiting for transfers between devices, exchange(): lax.all_to_all(rows.reshape(-1), AXES, 0, 0, tiled=True).reshape(rows.shape)  10.1 us
    ppermute x2, starting transfers between devices, shifted(): return lax.ppermute(value, AXES, pairs)  9.65 us
    pallas_call x1, Pallas kernels, local(): pl.pallas_call(field_kernel, out_shape=shape(DEVICES, 128), scratch_shape...  7.45 us
    unnamed x22, local copies, waits for them, and re-layouts  5.39 us
    pallas_call x1, Pallas kernels, local(): pl.pallas_call(pack_kernel, out_shape=(shape(CHUNKS * 128, 128), shape(1,...  2.71 us
    pallas_call x1, Pallas kernels, local(): pl.pallas_call(density_kernel, out_shape=shape(3 * LPTS, 128), in_specs=[...  1.47 us
    pallas_call x1, Pallas kernels, local(): pl.pallas_call(fiber_kernel, out_shape=shape(8, 256), scratch_shapes=[plt...  1.3 us
  transfers between devices with their start and end apart: 4, of which 2 were waited for; matrix products, arithmetic and copies ran while one was open for 0% of the time, Pallas kernels for 5%

profile of v5, /device:TPU:1, one launch (start us, length us, event | category | flops | bytes accessed | tf_op | source)
XLA Modules:
  0.0 56.5 jit_solution(7519289112394259327)
XLA Ops:
  0.0 0.0 copy-start.4
  0.0 0.0 copy-start.8
  0.0 2.7 %pack.1 = (f32[1920,128]{1,0:T(8,128)}, f32[1,512]{1,0:T(1,128)}) custom-call(f32[3,512]{1,0:T(4,128)} %pos_ref.1, f32[3,512]{1,0:T(4,128)} %force_ref.1, s32[1,512]{1,0:T(1,128)} %bitcast.16), custom_call_target="tpu_custom_call" | custom-call | flops 100000000 | bytes 1000000 | tf_op jit(solution)/shard_map/pack/pallas_call | solution.py:372
  2.7 11.5 %all-to-all-start = ((f32[128,1920,1]{1,2,0:T(1,128)}), f32[128,1920,1]{1,2,0:T(1,128)S(1)}, u32[]{:S(2)}, u32[]{:S(2)}) async-start(f32[128,1920,1]{1,2,0:T(1,128)} %bitcast.19), calls=%async_computation | async-start | bytes 1966080 | tf_op jit(solution)/shard_map/all_to_all | solution.py:362
  14.2 3.3 %collective-permute-start = (f32[3,2,128]{2,1,0:T(2,128)}, f32[3,2,128]{2,1,0:T(2,128)S(1)}, u32[]{:S(2)}, u32[]{:S(2)}) collective-permute-start(f32[3,2,128]{2,1,0:T(2,128)} %bitcast.13), channel_id=1, source_target_pairs={{0,1},{1,2},{2,3},{3,4},{4,5},{5,6},{6,7},{7,8},{8,9},{9,10},{10,1... | collective-permute-start | bytes 9224 | tf_op jit(solution)/shard_map/ppermute | solution.py:354
  17.5 6.4 %collective-permute-start.1 = (f32[3,2,128]{2,1,0:T(2,128)}, f32[3,2,128]{2,1,0:T(2,128)S(1)}, u32[]{:S(2)}, u32[]{:S(2)}) collective-permute-start(f32[3,2,128]{2,1,0:T(2,128)} %bitcast.14), channel_id=1, source_target_pairs={{1,0},{2,1},{3,2},{4,3},{5,4},{6,5},{7,6},{8,7},{9,8},{10,9},{11,1... | collective-permute-start | bytes 9224 | tf_op jit(solution)/shard_map/ppermute | solution.py:354
  23.9 0.0 copy-start
  23.9 2.3 %copy-done = f32[8,384,384]{2,1,0:T(8,128)S(1)} copy-done((f32[8,384,384]{2,1,0:T(8,128)S(1)}, f32[8,384,384]{2,1,0:T(8,128)}, u32[]{:S(2)}) %copy-start) | copy-done | bytes 4718616
  26.2 0.7 %copy-done.2 = f32[16,3,128]{2,0,1:T(8,128)S(1)} copy-done((f32[16,3,128]{2,0,1:T(8,128)S(1)}, f32[16,3,128]{2,0,1:T(8,128)}, u32[]{:S(2)}) %copy-start.2) | copy-done | bytes 24600
  27.0 0.7 %copy-done.3 = s32[16,27]{1,0:T(8,128)S(1)} copy-done((s32[16,27]{1,0:T(8,128)S(1)}, s32[16,27]{1,0:T(8,128)}, u32[]{:S(2)}) %copy-start.3) | copy-done | bytes 1752
  27.7 0.6 %prepare.1 = (bf16[512,512]{1,0:T(8,128)(2,1)S(1)}, bf16[512,512]{1,0:T(8,128)(2,1)S(1)}, f32[96,128]{1,0:T(8,128)S(1)}, f32[8,384,384]{2,1,0:T(8,128)S(1)}) custom-call(s32[16,27]{1,0:T(8,128)S(1)} %copy-done.3, f32[3,16,128]{2,1,0:T(8,128)S(1)} %bitcast.12, f32[8,384,384]{2,1,0:T(8,128)S(1)} %copy-done), custom_call_target="tpu_custom_call" | custom-call | flops 5000000 | bytes 10000000 | tf_op jit(solution)/shard_map/prepare/pallas_call | solution.py:386
  28.3 0.0 collective-permute-done.before_ref
  28.3 0.0 collective-permute-done.1.after_ref
  28.3 0.0 copy-done.4
  28.3 0.0 copy-done.8
  28.3 0.0 copy-done.9
  28.4 1.5 %density.1.density_ref = f32[96,128]{1,0:T(8,128)S(1)} custom-call(s32[16]{0:T(128)S(1)} %copy-done.8, s32[16]{0:T(128)S(1)} %copy-done.9, f32[3,2,128]{2,1,0:T(2,128)S(1)} %collective-permute-done.before_ref, f32[3,2,128]{2,1,0:T(2,128)S(1)} %bitcast.15, f32[3,2,128]{2,1,0:T(2,128)S(1)} %collective-permute-done.1.after_ref, ...), custom_call_target="tpu_custom_call" | custom-call | flops 1000000000 | bytes 5000000 | tf_op jit(solution)/shard_map/density/pallas_call | solution.py:408
  29.8 0.0 copy-start.5
  29.8 0.0 copy-start.6
  29.9 0.0 copy-start.7
  29.9 2.9 %all-to-all-done = f32[128,1920,1]{1,2,0:T(1,128)S(1)} async-done(((f32[128,1920,1]{1,2,0:T(1,128)}), f32[128,1920,1]{1,2,0:T(1,128)S(1)}, u32[]{:S(2)}, u32[]{:S(2)}) %all-to-all-start) | async-done | bytes 983072 | tf_op jit(solution)/shard_map/all_to_all | solution.py:362
  32.8 0.0 copy-done.10
  32.8 7.5 %field.1 = f32[128,128]{1,0:T(8,128)} custom-call(f32[1920,128]{1,0:T(8,128)S(1)} %bitcast.10, bf16[512,512]{1,0:T(8,128)(2,1)S(1)} %get-tuple-element.15.near_hot_ref, bf16[512,512]{1,0:T(8,128)(2,1)S(1)} %get-tuple-element.16.own_hot_ref, f32[96,128]{1,0:T(8,128)S(1)} %density.1.density_ref, f32[96,128]{1,0:T(8,128)S(1)} %copy-done.10), custom_call_target="tpu_custom_call" | custom-call | flops 1000000000 | bytes 2000000 | tf_op jit(solution)/shard_map/field/pallas_call | solution.py:420
  40.2 5.2 %all-to-all-start.1 = ((f32[128,128,1]{1,2,0:T(1,128)}), f32[128,128,1]{1,2,0:T(1,128)S(1)}, u32[]{:S(2)}, u32[]{:S(2)}) async-start(f32[128,128,1]{1,2,0:T(1,128)} %bitcast.6), calls=%async_computation.1 | async-start | bytes 131072 | tf_op jit(solution)/shard_map/all_to_all | solution.py:362
  45.4 0.0 copy-start.1
  45.4 1.6 %copy-done.1 = f32[8,256,256]{2,1,0:T(8,128)S(1)} copy-done((f32[8,256,256]{2,1,0:T(8,128)S(1)}, f32[8,256,256]{2,1,0:T(8,128)}, u32[]{:S(2)}) %copy-start.1) | copy-done | bytes 2097176
  47.0 1.0 %split.1.blocks_ref = bf16[2,8,256,256]{3,2,1,0:T(8,128)(2,1)S(1)} custom-call(f32[8,256,256]{2,1,0:T(8,128)S(1)} %copy-done.1), custom_call_target="tpu_custom_call" | custom-call | flops 2000000 | bytes 4000000 | tf_op jit(solution)/shard_map/split/pallas_call | solution.py:398
  48.0 7.2 %all-to-all-done.1 = f32[128,128,1]{1,2,0:T(1,128)S(1)} async-done(((f32[128,128,1]{1,2,0:T(1,128)}), f32[128,128,1]{1,2,0:T(1,128)S(1)}, u32[]{:S(2)}, u32[]{:S(2)}) %all-to-all-start.1) | async-done | bytes 65568 | tf_op jit(solution)/shard_map/all_to_all | solution.py:362
  55.2 0.0 copy-done.5
  55.2 0.0 copy-done.6
  55.2 0.0 copy-done.7
  55.3 1.3 %fiber.1 = f32[8,256]{1,0:T(8,128)} custom-call(f32[128,128]{1,0:T(8,128)S(1)} %bitcast.11, s32[1,512]{1,0:T(1,128)S(1)} %bitcast.17, f32[1,512]{1,0:T(1,128)S(1)} %copy-done.7, f32[1,512]{1,0:T(1,128)S(1)} %bitcast.18, bf16[2,8,256,256]{3,2,1,0:T(8,128)(2,1)S(1)} %split.1.blocks_ref), custom_call_target="tpu_custom_call" | custom-call | flops 100000000 | bytes 2000000 | tf_op jit(solution)/shard_map/fiber/pallas_call | solution.py:436
  (4 shorter events, 0.0 us)
Async XLA Ops:
  0.0 28.3 %copy-start.4 = (f32[2,3,128]{2,0,1:T(2,128)S(1)}, f32[2,3,128]{2,0,1:T(2,128)}, u32[]{:S(2)}) copy-start(f32[2,3,128]{2,0,1:T(2,128)} %param.17) | copy-start | bytes 9220
  0.0 28.3 %copy-start.8 = (s32[16]{0:T(128)S(1)}, s32[16]{0:T(128)}, u32[]{:S(2)}) copy-start(s32[16]{0:T(128)} %parent_ref.1) | copy-start | bytes 196
  0.0 28.3 %copy-start.9 = (s32[16]{0:T(128)S(1)}, s32[16]{0:T(128)}, u32[]{:S(2)}) copy-start(s32[16]{0:T(128)} %octant_ref.1) | copy-start | bytes 196
  2.7 30.1 %all-to-all-start = ((f32[128,1920,1]{1,2,0:T(1,128)}), f32[128,1920,1]{1,2,0:T(1,128)S(1)}, u32[]{:S(2)}, u32[]{:S(2)}) async-start(f32[128,1920,1]{1,2,0:T(1,128)} %bitcast.19), calls=%async_computation | async-start | bytes 1966080 | tf_op jit(solution)/shard_map/all_to_all | solution.py:362
  14.2 14.1 %collective-permute-start = (f32[3,2,128]{2,1,0:T(2,128)}, f32[3,2,128]{2,1,0:T(2,128)S(1)}, u32[]{:S(2)}, u32[]{:S(2)}) collective-permute-start(f32[3,2,128]{2,1,0:T(2,128)} %bitcast.13), channel_id=1, source_target_pairs={{0,1},{1,2},{2,3},{3,4},{4,5},{5,6},{6,7},{7,8},{8,9},{9,10},{10,1... | collective-permute-start | bytes 9224 | tf_op jit(solution)/shard_map/ppermute | solution.py:354
  17.5 10.8 %collective-permute-start.1 = (f32[3,2,128]{2,1,0:T(2,128)}, f32[3,2,128]{2,1,0:T(2,128)S(1)}, u32[]{:S(2)}, u32[]{:S(2)}) collective-permute-start(f32[3,2,128]{2,1,0:T(2,128)} %bitcast.14), channel_id=1, source_target_pairs={{1,0},{2,1},{3,2},{4,3},{5,4},{6,5},{7,6},{8,7},{9,8},{10,9},{11,1... | collective-permute-start | bytes 9224 | tf_op jit(solution)/shard_map/ppermute | solution.py:354
  23.9 2.3 %copy-start = (f32[8,384,384]{2,1,0:T(8,128)S(1)}, f32[8,384,384]{2,1,0:T(8,128)}, u32[]{:S(2)}) copy-start(f32[8,384,384]{2,1,0:T(8,128)} %maps_ref.1) | copy-start | bytes 14155780
  26.2 0.7 %copy-start.2 = (f32[16,3,128]{2,0,1:T(8,128)S(1)}, f32[16,3,128]{2,0,1:T(8,128)}, u32[]{:S(2)}) copy-start(f32[16,3,128]{2,0,1:T(8,128)} %param.16) | copy-start | bytes 73732
  27.0 0.7 %copy-start.3 = (s32[16,27]{1,0:T(8,128)S(1)}, s32[16,27]{1,0:T(8,128)}, u32[]{:S(2)}) copy-start(s32[16,27]{1,0:T(8,128)} %near_ref.1) | copy-start | bytes 5188
  27.7 5.1 %copy-start.10 = (f32[96,128]{1,0:T(8,128)S(1)}, f32[96,128]{1,0:T(8,128)}, u32[]{:S(2)}) copy-start(f32[96,128]{1,0:T(8,128)} %constant.2.clone.shell_ref) | copy-start | bytes 147460
  29.8 25.4 %copy-start.5 = (s32[512]{0:T(512)S(1)}, s32[512]{0:T(512)}, u32[]{:S(2)}) copy-start(s32[512]{0:T(512)} %param.15) | copy-start | bytes 6148
  29.8 25.4 %copy-start.6 = (f32[512]{0:T(512)S(1)}, f32[512]{0:T(512)}, u32[]{:S(2)}) copy-start(f32[512]{0:T(512)} %param.14) | copy-start | bytes 6148
  29.9 25.4 %copy-start.7 = (f32[1,512]{1,0:T(1,128)S(1)}, f32[1,512]{1,0:T(1,128)}, u32[]{:S(2)}) copy-start(f32[1,512]{1,0:T(1,128)} %get-tuple-element.20.rank_ref) | copy-start | bytes 6148
  40.2 15.0 %all-to-all-start.1 = ((f32[128,128,1]{1,2,0:T(1,128)}), f32[128,128,1]{1,2,0:T(1,128)S(1)}, u32[]{:S(2)}, u32[]{:S(2)}) async-start(f32[128,128,1]{1,2,0:T(1,128)} %bitcast.6), calls=%async_computation.1 | async-start | bytes 131072 | tf_op jit(solution)/shard_map/all_to_all | solution.py:362
  45.4 1.6 %copy-start.1 = (f32[8,256,256]{2,1,0:T(8,128)S(1)}, f32[8,256,256]{2,1,0:T(8,128)}, u32[]{:S(2)}) copy-start(f32[8,256,256]{2,1,0:T(8,128)} %blocks_ref.1) | copy-start | bytes 6291460
